TPU v7x, 256 devices: a whole 4x4x8 slice. The times are simulated.
256 devices in a mesh: lat: 16 (over z, core), lon: 8 (over x, y_hi), ens: 2 (over y_lo).
Axes of the slice: x: 4, y: 4 (y_hi: 2, y_lo: 2; y = y_hi * 2 + y_lo), z: 8, core: 2. Of those that a mesh axis runs over, the one named last changes fastest.
Arguments:
- state: bfloat16 [4, 96, 192, 768], P('ens', 'lat', 'lon'), parts along dimension 0, may hold values from -6 to 6
- spec_weight1: float32 [2, 8, 96, 96], P(None, 'lon'), may hold values from -0.4375 to 0.4375
- spec_bias1: float32 [2, 8, 96], P(None, 'lon'), may hold values from -0.6 to 0.6
- spec_weight2: float32 [2, 8, 96, 96], P(None, 'lon'), may hold values from -0.4375 to 0.4375
- spec_bias2: float32 [2, 8, 96], P(None, 'lon'), may hold values from -0.12 to 0.12
- norm1_gain: float32 [768], replicated, may hold values from 0.5 to 1.5
- norm1_bias: float32 [768], replicated, may hold values from -0.6 to 0.6
- norm2_gain: float32 [768], replicated, may hold values from 0.5 to 1.5
- norm2_bias: float32 [768], replicated, may hold values from -0.6 to 0.6
- fc1_weight: bfloat16 [768, 3072], replicated, may hold values from -0.21875 to 0.21875
- fc1_bias: float32 [3072], replicated, may hold values from -0.6 to 0.6
- fc2_weight: bfloat16 [3072, 768], replicated, may hold values from -0.109375 to 0.109375
- fc2_bias: float32 [768], replicated, may hold values from -0.6 to 0.6
- cotangent: bfloat16 [4, 96, 192, 768], P('ens', 'lat', 'lon'), parts along dimension 0, may hold values from -6 to 6
Outputs:
- advanced: bfloat16 [4, 96, 192, 768], P('ens', 'lat', 'lon'), parts along dimension 0
- sensitivity: bfloat16 [4, 96, 192, 768], P('ens', 'lat', 'lon'), parts along dimension 0
There are 2 independent parts, one for each index of `ens`. A program takes and returns all parts, laid end to end along the dimension named above; an argument that names none is the same for every part. Nothing has to cross between parts.
All inputs are finite; a program needn't handle non-finite values.
Results may differ from a plain program's by a relative error of at most 0.0085.
Values may be sent and summed in bfloat16 or wider, within the bound.
A program may use at most 128 MiB of HBM per device.

v0:
```python
import math

import jax
import jax.numpy as jnp
import numpy as np
from jax import lax
from jax.experimental import pallas as pl
from jax.experimental.pallas import tpu as pltpu
from jax.sharding import PartitionSpec as P

EPSILON = 1e-06
THRESHOLD = 0.01
F32 = jnp.float32
BF16 = jnp.bfloat16

NP = 16
NJ = 8
R = 6
C = 24
TOK = R * C
KS = 6
H = NP * R
W = NJ * C
BS = 96
D = 768
FF = 3072
HC = 512
ROWS = 2 * KS * H

roll = pltpu.roll


def tables():
    def cs(rows, cols, modulus):
        angle = 2.0 * np.pi * (np.outer(rows, cols) % modulus) / modulus
        return np.cos(angle) / math.sqrt(modulus), np.sin(angle) / math.sqrt(modulus)

    w = np.arange(W)
    cosine, sine = cs(w, np.arange(W // 2), W)
    parity = (1.0 - 2.0 * (w % 2)) / math.sqrt(W)
    ahead = np.zeros((NP, 16, W))
    even = np.zeros((W, NP, 16))
    odd = np.zeros((W, NP, 16))
    for p in range(NP):
        for kc in range(12):
            c, k = divmod(kc, KS)
            f = p * KS + k
            if c == 0:
                row, back = cosine[:, f], (2.0 if f else 1.0) * cosine[:, f]
            else:
                row, back = (-sine[:, f], -2.0 * sine[:, f]) if f else (parity, parity)
            ahead[p, kc] = row
            if kc < 8:
                even[:, p, kc] = back
                odd[:, p, kc] = back
            else:
                ahead[p, kc + 4] = row
                even[:, p, kc] = back
                odd[:, p, kc + 4] = back
    ahead = ahead.reshape(NP * 16, W)
    even = even.reshape(W, NP * 16)
    odd = odd.reshape(W, NP * 16)
    g = np.arange(H)
    co, si = cs(g, g, H)
    zero = np.zeros_like(co)
    fwd = np.block([[co, si], [-si, co]])
    inv = np.block([[co, -si], [si, co]])
    fwd0 = np.stack(
        [
            np.block([[co, si], [-si, co], [co, si], [si, -co]]),
            np.block([[co, zero], [-si, zero], [zero, co], [zero, -si]]),
        ]
    )
    inv0 = np.stack(
        [
            0.5 * np.block([[co, -si, co, si], [si, co, si, -co]]),
            np.block([[co, -si, zero, zero], [zero, zero, co, -si]]),
        ]
    )
    return [ahead, even, odd, fwd, 0.5 * inv, fwd0, inv0]


def split_table(table):
    high = np.asarray(table, np.float32).astype(jnp.bfloat16)
    low = (np.asarray(table, np.float64) - high.astype(np.float64)).astype(np.float32).astype(jnp.bfloat16)
    return np.stack([high, low])


def dot(a, b):
    return jnp.dot(a, b, preferred_element_type=F32)


def dot_nt(a, b):
    return lax.dot_general(a, b, (((1,), (1,)), ((), ())), preferred_element_type=F32)


def table_dot(high, low, x):
    x = x.astype(BF16)
    return dot(high, x) + dot(low, x)


def lanes():
    return lax.broadcasted_iota(jnp.int32, (1, 128), 1)


def layer_norm(values):
    average = jnp.mean(values, axis=-1, keepdims=True)
    centred = values - average
    inverse = lax.rsqrt(jnp.mean(centred * centred, axis=-1, keepdims=True) + EPSILON)
    return centred * inverse, inverse


def norm_backward(gradient, gain, normed, inverse):
    scaled = gradient * gain
    return inverse * (
        scaled
        - jnp.mean(scaled, axis=-1, keepdims=True)
        - normed * jnp.mean(scaled * normed, axis=-1, keepdims=True)
    )


def cumulative(values):
    return 0.5 * (1.0 + lax.erf(values * 0.7071067811865476))


def density(values):
    return jnp.exp(-0.5 * values * values) * 0.3989422804014327


def feature_block(tile, b):
    t, o = divmod(BS * b, 128)
    if o == 0:
        return tile(t)
    first = roll(tile(t), 128 - o, 1)
    if o == 32:
        return first
    return jnp.where(lanes() < 128 - o, first, roll(tile(t + 1), 128 - o, 1))


def joined_blocks(blocks):
    lane = lanes()
    tiles = []
    for q in (0, 4):
        one, two, three = roll(blocks[q + 1], 96, 1), roll(blocks[q + 2], 64, 1), roll(blocks[q + 3], 32, 1)
        tiles += [
            jnp.where(lane < 96, blocks[q], one),
            jnp.where(lane < 64, one, two),
            jnp.where(lane < 32, two, three),
        ]
    return jnp.concatenate(tiles, axis=1)


def pack_lon(m):
    lane = lanes()
    extra = m[112:144]
    parts = [jnp.where(lane < 96, m[32 * i : 32 * i + 32], roll(extra, 96 - 32 * i, 1) if i < 3 else extra) for i in range(3)]
    return jnp.concatenate(parts + [m[96:112]], axis=0)


def unpack_lon(m):
    lane = lanes()
    extra = jnp.where(
        lane < 32, roll(m[0:32], 32, 1), jnp.where(lane < 64, roll(m[32:64], 64, 1), roll(m[64:96], 96, 1))
    )
    return jnp.concatenate([m, extra], axis=0)


def pack_lat(t):
    lane = lanes()
    out = []
    for i in range(R):
        shift = 96 - 32 * (i % 3)
        out.append(jnp.where(lane < 96, t[i], roll(t[7 + i // 3], shift, 1)))
    return jnp.concatenate(out + [t[6]], axis=0)


def unpack_lat(m):
    lane = lanes()
    t = [m[8 * i : 8 * i + 8] for i in range(7)]
    for e in range(2):
        a, b, c = t[3 * e : 3 * e + 3]
        t.append(jnp.where(lane < 32, roll(a, 32, 1), jnp.where(lane < 64, roll(b, 64, 1), roll(c, 96, 1))))
    return t


def unpack_rows(recv, wide, peers=range(NJ)):
    for j in peers:
        m = unpack_lon(recv(j).astype(F32))
        for r in range(R):
            wide[C * j : C * j + C, 128 * r : 128 * r + 128] = m[C * r : C * r + C]


def width_ahead(recv, wide, tall, ahead, put):
    unpack_rows(recv, wide)
    tall[...] = table_dot(ahead[0], ahead[1], wide[...])
    upper = lax.broadcasted_iota(jnp.int32, (8, 1), 0) < 4
    for p in range(NP):
        def rows(r, at):
            return tall[16 * p + at : 16 * p + at + 8, 128 * r : 128 * r + 128]
        t = [rows(r, 0) for r in range(R)]
        t += [jnp.where(upper, rows(2 * i, 8), rows(2 * i + 1, 8)) for i in range(3)]
        put(p, pack_lat(t))


def slot_rows(kc, eights, fours):
    if kc < 8:
        return eights, pl.ds(kc, H, stride=8)
    return fours, pl.ds(kc - 8, H, stride=4)


def height_ahead(recv, eights, fours, wide, spec, fwd, fwd0):
    for p in range(NP):
        t = unpack_lat(recv(p).astype(F32))
        eights[48 * p : 48 * p + 48, :] = jnp.concatenate(t[:6], axis=0)
        fours[24 * p : 24 * p + 24, :] = jnp.concatenate(t[6:], axis=0)
    for c in range(2):
        for k in range(KS):
            ref, rows = slot_rows(c * KS + k, eights, fours)
            wide[H * c : H * c + H, 128 * k : 128 * k + 128] = ref[rows, :]
    zero = table_dot(fwd0[0], fwd0[1], wide[:, 0:128])
    rest = table_dot(fwd[0], fwd[1], wide[:, 128:])
    half = KS * H
    spec[0:H, 0:128] = zero[0:H]
    spec[0:H, 128:256] = zero[H : 2 * H]
    spec[half : half + H, 0:128] = zero[2 * H : 3 * H]
    spec[half : half + H, 128:256] = zero[3 * H :]
    for k in range(1, KS):
        real, imag = rest[0:H, 128 * (k - 1) : 128 * k], rest[H:, 128 * (k - 1) : 128 * k]
        spec[H * k : H * k + H, 0:128] = real
        spec[H * k : H * k + H, 128:256] = imag
        spec[half + H * k : half + H * k + H, 0:128] = real
        spec[half + H * k : half + H * k + H, 128:256] = -imag


def height_back(spec, eights, fours, wide, first, inv, inv0, put):
    half = KS * H
    for i, (at, lane) in enumerate(((0, 0), (0, 128), (half, 0), (half, 128))):
        first[H * i : H * i + H, :] = spec[at : at + H, lane : lane + 128]
    for k in range(1, KS):
        low = spec[H * k : H * k + H, :]
        high = spec[half + H * k : half + H * k + H, :]
        wide[0:H, 128 * k : 128 * k + 128] = low[:, 0:128] + high[:, 0:128]
        wide[H : 2 * H, 128 * k : 128 * k + 128] = low[:, 128:] - high[:, 128:]
    zero = table_dot(inv0[0], inv0[1], first[...])
    rest = table_dot(inv[0], inv[1], wide[:, 128:])
    for c in range(2):
        for k in range(KS):
            ref, rows = slot_rows(c * KS + k, eights, fours)
            values = zero[H * c : H * c + H] if k == 0 else rest[H * c : H * c + H, 128 * (k - 1) : 128 * k]
            ref[rows, :] = values
    for p in range(NP):
        t = [eights[48 * p + 8 * i : 48 * p + 8 * i + 8, :] for i in range(6)]
        t += [fours[24 * p + 8 * i : 24 * p + 8 * i + 8, :] for i in range(3)]
        put(p, pack_lat(t))


def width_back(recv, tall, even, odd, put):
    for p in range(NP):
        t = unpack_lat(recv(p).astype(F32))
        for r in range(R):
            at = 128 * (r // 2) + 384 * (r % 2)
            tall[16 * p : 16 * p + 8, at : at + 128] = t[r]
            tall[16 * p + 8 : 16 * p + 16, at : at + 128] = t[6 + r // 2]
    fields = (table_dot(even[0], even[1], tall[:, 0:384]), table_dot(odd[0], odd[1], tall[:, 384:768]))
    for j in range(NJ):
        m = [fields[r % 2][C * j : C * j + C, 128 * (r // 2) : 128 * (r // 2) + 128] for r in range(R)]
        put(j, pack_lon(jnp.concatenate(m, axis=0)))


def gathered(recv):
    return joined_blocks([unpack_lon(recv(b).astype(F32))[:, 0:128] for b in range(NJ)])


def matrix_dot(values, matrix):
    return dot(values.astype(BF16), matrix[0])


def matrix_dot_nt(values, matrix):
    return dot_nt(values.astype(BF16), matrix[0])


CHUNK = 192


def spectral_ahead(loop, spec, first_pre, squares, mat1, bias1, mat2, bias2):
    def step(i):
        rows = pl.ds(pl.multiple_of(i * CHUNK, CHUNK), CHUNK)
        pre = matrix_dot(spec[rows, :], mat1) + bias1[...]
        first_pre[rows, :] = pre
        second = matrix_dot(pre * cumulative(pre), mat2) + bias2[...]
        slope = jnp.tanh(second * (1.0 / THRESHOLD))
        squares[rows, :] = slope * slope
        spec[rows, :] = second - THRESHOLD * slope
    loop(ROWS // CHUNK, step)


def spectral_slopes(loop, first_pre):
    def step(i):
        rows = pl.ds(pl.multiple_of(i * CHUNK, CHUNK), CHUNK)
        pre = first_pre[rows, :]
        first_pre[rows, :] = cumulative(pre) + pre * density(pre)
    loop(ROWS // CHUNK, step)


def spectral_adjoint(loop, spec, slopes, squares, mat1, mat2):
    def step(i):
        rows = pl.ds(pl.multiple_of(i * CHUNK, CHUNK), CHUNK)
        grad = matrix_dot_nt(spec[rows, :] * squares[rows, :], mat2)
        spec[rows, :] = matrix_dot_nt(grad * slopes[rows, :], mat1)
    loop(ROWS // CHUNK, step)


def fill_matrix(out, weight):
    out[...] = jnp.zeros_like(out)
    real, imag = weight[0, 0], weight[1, 0]
    out[0, 0:BS, 0:BS] = real.astype(BF16)
    out[0, 0:BS, 128 : 128 + BS] = imag.astype(BF16)
    out[0, 128 : 128 + BS, 0:BS] = (-imag).astype(BF16)
    out[0, 128 : 128 + BS, 128 : 128 + BS] = real.astype(BF16)


def fill_bias(out, bias):
    out[...] = jnp.zeros_like(out)
    out[0:1, 0:BS] = bias[0]
    out[0:1, 128 : 128 + BS] = bias[1]


def token_ahead(loop, mixed, cot, held, fc1, bias1, gain2, shift2, hidden, gh, acc):
    normed, inverse = layer_norm(mixed)
    v = (normed * gain2 + shift2).astype(BF16)
    acc[...] = jnp.zeros_like(acc)

    def step(n):
        cols = pl.ds(pl.multiple_of(n * HC, HC), HC)
        pre = dot(v, fc1[:, cols]) + bias1[:, cols]
        phi = cumulative(pre)
        hidden[held, cols] = (pre * phi).astype(BF16)
        grad = (gh[held, cols] * (phi + pre * density(pre))).astype(BF16)
        acc[...] += dot_nt(grad, fc1[:, cols])
    loop(FF // HC, step)
    return (cot + norm_backward(acc[...], gain2, normed, inverse)).astype(BF16).astype(F32)


def kernel(
    state, weight1, bias_1, weight2, bias_2, gain1, shift1, gain2, shift2, fc1_hbm, fc1_bias, fc2_hbm, fc2_bias, cotangent,
    ahead, even, odd, fwd, inv, fwd0_both, inv0_both,
    advanced, sensitivity,
    fc1, fc2, lon_send, lon_recv, lat_send, lat_recv, lowered, mixed, grads, hidden, gh, acc,
    wide, tall, eights, fours, first, spec, first_pre, squares, mat1, mat2, bias1, bias2, fwd0, inv0,
    load_sem, lon_send_sem, lon_recv_sem, lat_send_sem, lat_recv_sem,
):
    p = lax.axis_index("lat")
    j = lax.axis_index("lon")

    def loop(count, body):
        lax.fori_loop(0, count, lambda i, _: (body(i), 0)[1], 0)

    barrier = pltpu.get_barrier_semaphore()
    for d in range(1, NP):
        pl.semaphore_signal(barrier, inc=1, device_id={"lat": lax.rem(p + d, NP)}, device_id_type=pl.DeviceIdType.MESH)
    for d in range(1, NJ):
        pl.semaphore_signal(barrier, inc=1, device_id={"lon": lax.rem(j + d, NJ)}, device_id_type=pl.DeviceIdType.MESH)
    load2 = pltpu.make_async_copy(fc2_hbm, fc2, load_sem.at[0])
    load1 = pltpu.make_async_copy(fc1_hbm, fc1, load_sem.at[1])
    load2.start()
    load1.start()

    def sending(x, s, axis):
        e = 2 * x + s
        if axis == "lon":
            return lon_send, lon_recv, lon_send_sem, lon_recv_sem, e, NJ, j
        return lat_send, lat_recv, lat_send_sem, lat_recv_sem, e, NP, p

    def putter(x, s, axis):
        send, recv, _, _, e, n, me = sending(x, s, axis)

        def put(to, values):
            send[e, to] = values.astype(BF16)
        return put

    def copy(x, s, axis, to):
        send, recv, send_sem, recv_sem, e, n, me = sending(x, s, axis)
        return pltpu.make_async_remote_copy(
            src_ref=send.at[e, to],
            dst_ref=recv.at[e, me],
            send_sem=send_sem.at[e],
            recv_sem=recv_sem.at[e],
            device_id={axis: to},
            device_id_type=pl.DeviceIdType.MESH,
        )

    def go(x, s, axis):
        send, recv, _, _, e, n, me = sending(x, s, axis)
        for i in range(1, n):
            d = n - i // 2 if i % 2 else i // 2
            d = (i + 1) // 2 if i % 2 else n - i // 2
            copy(x, s, axis, lax.rem(me + d, n)).start()
        recv[e, me] = send[e, me]

    def all_but_one(x, s, axis):
        send, recv, send_sem, recv_sem, e, n, me = sending(x, s, axis)
        return pltpu.make_async_remote_copy(
            src_ref=send.at[e, pl.ds(0, n - 1)],
            dst_ref=recv.at[e, pl.ds(0, n - 1)],
            send_sem=send_sem.at[e],
            recv_sem=recv_sem.at[e],
            device_id={axis: lax.rem(me + 1, n)},
            device_id_type=pl.DeviceIdType.MESH,
        )

    def arrived(x, s, axis):
        all_but_one(x, s, axis).wait_recv()
        _, recv, _, _, e, _, _ = sending(x, s, axis)
        return lambda k: recv[e, k]

    def tokens(ref, s):
        return jnp.concatenate([ref[s, r].astype(F32) for r in range(R)], axis=0)

    def out_tokens(ref, s, values):
        for r in range(R):
            ref[s, r] = values[C * r : C * r + C].astype(BF16)

    def held(s):
        return pl.ds(TOK * s, TOK)

    def send_tokens(x, s, ref):
        put = putter(x, s, "lon")
        for b in range(NJ):
            put(b, pack_lon(feature_block(lambda t: ref[s, :, 128 * t : 128 * t + 128], b)))

    for s in range(2):
        normed, _ = layer_norm(tokens(state, s))
        lowered[s] = (normed * gain1[...] + shift1[...]).astype(BF16).astype(F32)
        send_tokens(0, s, lowered)
        if s == 0:
            pl.semaphore_wait(barrier, NP + NJ - 2)
        go(0, s, "lon")
    fill_matrix(mat1, weight1)
    fill_matrix(mat2, weight2)
    fill_bias(bias1, bias_1)
    fill_bias(bias2, bias_2)
    packed = p == 0
    fwd0[...] = jnp.where(packed, fwd0_both[1], fwd0_both[0])
    inv0[...] = jnp.where(packed, inv0_both[1], inv0_both[0])

    for s in range(2):
        width_ahead(arrived(0, s, "lon"), wide, tall, ahead, putter(0, s, "lat"))
        go(0, s, "lat")

    load2.wait()
    cots = jnp.concatenate([tokens(cotangent, s) for s in range(2)], axis=0).astype(BF16)

    def cot_step(n):
        cols = pl.ds(pl.multiple_of(n * HC, HC), HC)
        gh[:, cols] = dot_nt(cots, fc2[cols, :])
    loop(FF // HC, cot_step)

    for s in range(2):
        height_ahead(arrived(0, s, "lat"), eights, fours, wide, spec, fwd, fwd0)
        spectral_ahead(loop, spec, first_pre.at[s], squares.at[s], mat1, bias1, mat2, bias2)
        height_back(spec, eights, fours, wide, first, inv, inv0, putter(1, s, "lat"))
        go(1, s, "lat")
    for s in range(2):
        spectral_slopes(loop, first_pre.at[s])
    load1.wait()
    for s in range(2):
        width_back(arrived(1, s, "lat"), tall, even, odd, putter(1, s, "lon"))
        go(1, s, "lon")
    for s in range(2):
        filtered = gathered(arrived(1, s, "lon"))
        mixed[s] = (filtered + lowered[s] + tokens(state, s)).astype(BF16).astype(F32)
        grads[s] = token_ahead(
            loop, mixed[s], tokens(cotangent, s), held(s), fc1, fc1_bias, gain2[...], shift2[...], hidden, gh, acc
        )
        send_tokens(2, s, grads)
        go(2, s, "lon")

    def advance(s):
        for n in range(D // 256):
            cols = slice(256 * n, 256 * n + 256)
            values = dot(hidden[TOK * s : TOK * s + TOK, :], fc2[:, cols]) + fc2_bias[:, cols] + mixed[s, :, cols]
            for r in range(R):
                advanced[s, r, :, cols] = values[C * r : C * r + C].astype(BF16)

    for s in range(2):
        width_ahead(arrived(2, s, "lon"), wide, tall, ahead, putter(2, s, "lat"))
        go(2, s, "lat")
    for s in range(2):
        advance(s)
    for s in range(2):
        height_ahead(arrived(2, s, "lat"), eights, fours, wide, spec, fwd, fwd0)
        spectral_adjoint(loop, spec, first_pre.at[s], squares.at[s], mat1, mat2)
        height_back(spec, eights, fours, wide, first, inv, inv0, putter(3, s, "lat"))
        go(3, s, "lat")
    for s in range(2):
        width_back(arrived(3, s, "lat"), tall, even, odd, putter(3, s, "lon"))
        go(3, s, "lon")
    for s in range(2):
        grad = grads[s]
        grad_lowered = gathered(arrived(3, s, "lon")) + grad
        normed, inverse = layer_norm(tokens(state, s))
        out_tokens(sensitivity, s, grad + norm_backward(grad_lowered, gain1[...], normed, inverse))
    for x in range(4):
        for s in range(2):
            all_but_one(x, s, "lon").wait_send()
            all_but_one(x, s, "lat").wait_send()


def shards(
    state, spec_weight1, spec_bias1, spec_weight2, spec_bias2, norm1_gain, norm1_bias, norm2_gain, norm2_bias,
    fc1_weight, fc1_bias, fc2_weight, fc2_bias, cotangent,
):
    vmem = pl.BlockSpec(memory_space=pltpu.VMEM)
    hbm = pl.BlockSpec(memory_space=pl.ANY)
    names = [jnp.asarray(split_table(t)) if t.ndim == 2 else jnp.asarray(np.stack([split_table(x) for x in t])) for t in tables()]
    row = lambda a: a.reshape(1, -1)
    operands = [
        state, spec_weight1, spec_bias1, spec_weight2, spec_bias2, row(norm1_gain), row(norm1_bias), row(norm2_gain),
        row(norm2_bias), fc1_weight, row(fc1_bias), fc2_weight, row(fc2_bias), cotangent, *names,
    ]
    specs = [hbm if i in (9, 11) else vmem for i in range(len(operands))]
    out = jax.ShapeDtypeStruct(state.shape, BF16)
    return pl.pallas_call(
        kernel,
        out_shape=(out, out),
        in_specs=specs,
        out_specs=(vmem, vmem),
        scratch_shapes=[
            pltpu.VMEM((D, FF), BF16),
            pltpu.VMEM((FF, D), BF16),
            pltpu.VMEM((8, NJ, 112, 128), BF16),
            pltpu.VMEM((8, NJ, 112, 128), BF16),
            pltpu.VMEM((8, NP, 56, 128), BF16),
            pltpu.VMEM((8, NP, 56, 128), BF16),
            pltpu.VMEM((2, TOK, D), F32),
            pltpu.VMEM((2, TOK, D), F32),
            pltpu.VMEM((2, TOK, D), F32),
            pltpu.VMEM((2 * TOK, FF), BF16),
            pltpu.VMEM((2 * TOK, FF), F32),
            pltpu.VMEM((TOK, D), F32),
            pltpu.VMEM((W, D), F32),
            pltpu.VMEM((16 * NP, D), F32),
            pltpu.VMEM((8 * H, 128), F32),
            pltpu.VMEM((4 * H, 128), F32),
            pltpu.VMEM((4 * H, 128), F32),
            pltpu.VMEM((ROWS, 256), F32),
            pltpu.VMEM((2, ROWS, 256), F32),
            pltpu.VMEM((2, ROWS, 256), F32),
            pltpu.VMEM((1, 256, 256), BF16),
            pltpu.VMEM((1, 256, 256), BF16),
            pltpu.VMEM((1, 256), F32),
            pltpu.VMEM((1, 256), F32),
            pltpu.VMEM((2, 4 * H, 2 * H), BF16),
            pltpu.VMEM((2, 2 * H, 4 * H), BF16),
            pltpu.SemaphoreType.DMA((2,)),
            pltpu.SemaphoreType.DMA((8,)),
            pltpu.SemaphoreType.DMA((8,)),
            pltpu.SemaphoreType.DMA((8,)),
            pltpu.SemaphoreType.DMA((8,)),
        ],
        compiler_params=pltpu.CompilerParams(
            collective_id=0, has_side_effects=True, vmem_limit_bytes=60 * 1024 * 1024
        ),
        name="block",
    )(*operands)


def solution(mesh):
    in_specs = (
        P("ens", "lat", "lon", None),
        P(None, "lon", None, None),
        P(None, "lon", None),
        P(None, "lon", None, None),
        P(None, "lon", None),
        P(), P(), P(), P(), P(), P(), P(), P(),
        P("ens", "lat", "lon", None),
    )
    out_specs = (P("ens", "lat", "lon", None), P("ens", "lat", "lon", None))
    return jax.shard_map(shards, mesh=mesh, in_specs=in_specs, out_specs=out_specs, check_vma=False)
```

profile of v0, /device:TPU:1, one launch (start us, length us, event | category | flops | bytes accessed | tf_op | source)
XLA Modules:
  0.0 100.1 jit_solution(8622245864315823563)
XLA Ops:
  0.6 1.3 %reshape.22.gain1 = f32[1,768]{1,0:T(1,128)} reshape(f32[768]{0:T(1024)} %param.26) | data formatting | bytes 6144 | tf_op jit(solution)/shard_map/reshape | solution.py:516
  1.9 1.3 %reshape.23.shift1 = f32[1,768]{1,0:T(1,128)} reshape(f32[768]{0:T(1024)} %param.27) | data formatting | bytes 6144 | tf_op jit(solution)/shard_map/reshape | solution.py:516
  3.2 1.3 %reshape.24.gain2 = f32[1,768]{1,0:T(1,128)} reshape(f32[768]{0:T(1024)} %param.28) | data formatting | bytes 6144 | tf_op jit(solution)/shard_map/reshape | solution.py:516
  4.4 1.3 %reshape.25.shift2 = f32[1,768]{1,0:T(1,128)} reshape(f32[768]{0:T(1024)} %param.29) | data formatting | bytes 6144 | tf_op jit(solution)/shard_map/reshape | solution.py:516
  5.7 1.3 %reshape.27.fc2_bias = f32[1,768]{1,0:T(1,128)} reshape(f32[768]{0:T(1024)} %param.33) | data formatting | bytes 6144 | tf_op jit(solution)/shard_map/reshape | solution.py:516
  7.0 89.5 %block.1 = (bf16[2,6,24,768]{3,2,1,0:T(8,128)(2,1)}, bf16[2,6,24,768]{3,2,1,0:T(8,128)(2,1)}) custom-call(bf16[2,6,24,768]{3,2,1,0:T(8,128)(2,1)} %state.1, f32[2,1,96,96]{3,2,1,0:T(8,128)} %weight1.1, f32[2,1,96]{2,1,0:T(1,128)} %bias_1.1, f32[2,1,96,96]{3,2,1,0:T(8,128)} %weight2.1, f32[2,1,96]{2,1,0:T(1,128)} %bias_2.1, f32[1,768]{1,0:T(1,128)} %reshape.22.gain1, ...), custom_call_target="tpu_custom_call" | custom-call | tf_op jit(solution)/shard_map/block/pallas_call | solution.py:523
  96.5 1.8 %copy.25 = bf16[2,6,24,768]{3,2,1,0:T(8,128)(2,1)} copy(bf16[2,6,24,768]{3,2,1,0:T(8,128)(2,1)} %get-tuple-element.4) | data formatting | bytes 884736
  98.3 1.8 %copy.26 = bf16[2,6,24,768]{3,2,1,0:T(8,128)(2,1)} copy(bf16[2,6,24,768]{3,2,1,0:T(8,128)(2,1)} %get-tuple-element.5) | data formatting | bytes 884736
where the time goes:
time: 100 us
  Pallas kernels  89.5 us (90%)
  local copies, waits for them, and re-layouts  9.97 us (10%)
    pallas_call x1, Pallas kernels, shards(): pl.pallas_call(kernel, out_shape=(out, out), in_specs=specs, out_specs=(v...  89.5 us
    reshape x5, local copies, waits for them, and re-layouts, shards(): row = lambda a: a.reshape(1, -1)  6.36 us
    unnamed x2, local copies, waits for them, and re-layouts  3.61 us

commit v1 on v0

v1 whole, which is shorter than its diff:
```python
import math

import jax
import jax.numpy as jnp
import numpy as np
from jax import lax
from jax.experimental import pallas as pl
from jax.experimental.pallas import tpu as pltpu
from jax.sharding import PartitionSpec as P

EPSILON = 1e-06
THRESHOLD = 0.01
F32 = jnp.float32
BF16 = jnp.bfloat16

NP = 16
NJ = 8
R = 6
C = 24
TOK = R * C
KS = 6
H = NP * R
W = NJ * C
BS = 96
D = 768
FF = 3072
HC = 512
ROWS = 2 * KS * H
FIRST, MIDDLE, LAST = [0, 5, 6], [1, 2, 3, 4, 7, 8, 10, 12, 13, 14, 15, 16, 17, 18], [11, 9]

roll = pltpu.roll


def tables():
    def cs(rows, cols, modulus):
        angle = 2.0 * np.pi * (np.outer(rows, cols) % modulus) / modulus
        return np.cos(angle) / math.sqrt(modulus), np.sin(angle) / math.sqrt(modulus)

    w = np.arange(W)
    cosine, sine = cs(w, np.arange(W // 2), W)
    parity = (1.0 - 2.0 * (w % 2)) / math.sqrt(W)
    ahead = np.zeros((NP, 16, W))
    even = np.zeros((W, NP, 16))
    odd = np.zeros((W, NP, 16))
    for p in range(NP):
        for kc in range(12):
            c, k = divmod(kc, KS)
            f = p * KS + k
            if c == 0:
                row, back = cosine[:, f], (2.0 if f else 1.0) * cosine[:, f]
            else:
                row, back = (-sine[:, f], -2.0 * sine[:, f]) if f else (parity, parity)
            ahead[p, kc] = row
            if kc < 8:
                even[:, p, kc] = back
                odd[:, p, kc] = back
            else:
                ahead[p, kc + 4] = row
                even[:, p, kc] = back
                odd[:, p, kc + 4] = back
    ahead = ahead.reshape(NP * 16, W)
    even = even.reshape(W, NP * 16)
    odd = odd.reshape(W, NP * 16)
    g = np.arange(H)
    co, si = cs(g, g, H)
    fwd = np.block([[co, si], [-si, co]])
    inv = 0.5 * np.block([[co, -si], [si, co]])
    return [split_table(ahead), split_table(fwd), rounded(even), rounded(odd), rounded(inv)]


def rounded(table):
    return np.asarray(table, np.float32).astype(jnp.bfloat16)


def split_table(table):
    high = np.asarray(table, np.float32).astype(jnp.bfloat16)
    low = (np.asarray(table, np.float64) - high.astype(np.float64)).astype(np.float32).astype(jnp.bfloat16)
    return np.stack([high, low])


def dot(a, b):
    return jnp.dot(a, b, preferred_element_type=F32)


def dot_nt(a, b):
    return lax.dot_general(a, b, (((1,), (1,)), ((), ())), preferred_element_type=F32)


def table_dot(table, x):
    x = x.astype(BF16)
    if len(table.shape) == 2:
        return dot(table[...], x)
    return dot(table[0], x) + dot(table[1], x)


def row(ref):
    return ref[...].reshape(1, -1)


def lanes():
    return lax.broadcasted_iota(jnp.int32, (1, 128), 1)


def layer_norm(values):
    average = jnp.mean(values, axis=-1, keepdims=True)
    centred = values - average
    inverse = lax.rsqrt(jnp.mean(centred * centred, axis=-1, keepdims=True) + EPSILON)
    return centred * inverse, inverse


def norm_backward(gradient, gain, normed, inverse):
    scaled = gradient * gain
    return inverse * (
        scaled
        - jnp.mean(scaled, axis=-1, keepdims=True)
        - normed * jnp.mean(scaled * normed, axis=-1, keepdims=True)
    )


def cumulative(values):
    return 0.5 * (1.0 + lax.erf(values * 0.7071067811865476))


def density(values):
    return jnp.exp(-0.5 * values * values) * 0.3989422804014327


def feature_block(tile, b):
    t, o = divmod(BS * b, 128)
    if o == 0:
        return tile(t)
    first = roll(tile(t), 128 - o, 1)
    if o == 32:
        return first
    return jnp.where(lanes() < 128 - o, first, roll(tile(t + 1), 128 - o, 1))


def joined_blocks(blocks):
    lane = lanes()
    tiles = []
    for q in (0, 4):
        one, two, three = roll(blocks[q + 1], 96, 1), roll(blocks[q + 2], 64, 1), roll(blocks[q + 3], 32, 1)
        tiles += [
            jnp.where(lane < 96, blocks[q], one),
            jnp.where(lane < 64, one, two),
            jnp.where(lane < 32, two, three),
        ]
    return jnp.concatenate(tiles, axis=1)


def pack_lon(m):
    lane = lanes()
    extra = m[112:144]
    parts = [jnp.where(lane < 96, m[32 * i : 32 * i + 32], roll(extra, 96 - 32 * i, 1) if i < 3 else extra) for i in range(3)]
    return jnp.concatenate(parts + [m[96:112]], axis=0)


def unpack_lon(m):
    lane = lanes()
    extra = jnp.where(
        lane < 32, roll(m[0:32], 32, 1), jnp.where(lane < 64, roll(m[32:64], 64, 1), roll(m[64:96], 96, 1))
    )
    return jnp.concatenate([m, extra], axis=0)


def pack_lat(t):
    lane = lanes()
    out = []
    for i in range(R):
        shift = 96 - 32 * (i % 3)
        out.append(jnp.where(lane < 96, t[i], roll(t[7 + i // 3], shift, 1)))
    return jnp.concatenate(out + [t[6]], axis=0)


def unpack_lat(m):
    lane = lanes()
    t = [m[8 * i : 8 * i + 8] for i in range(7)]
    for e in range(2):
        a, b, c = t[3 * e : 3 * e + 3]
        t.append(jnp.where(lane < 32, roll(a, 32, 1), jnp.where(lane < 64, roll(b, 64, 1), roll(c, 96, 1))))
    return t


def at(index, size, count=None, offset=0):
    return pl.ds(pl.multiple_of(index * size + offset, 8), count or size)


def width_ahead(froms, recv, wide, tall, ahead, tos, put):
    for group in froms:
        recv.wait(group)
        for j in group:
            m = unpack_lon(recv(j).astype(F32))
            for r in range(R):
                wide[at(j, C), 128 * r : 128 * r + 128] = m[C * r : C * r + C]
    tall[...] = table_dot(ahead, wide[...])
    upper = lax.broadcasted_iota(jnp.int32, (8, 1), 0) < 4
    for group in tos:
        for p in group:
            def rows(r, offset):
                return tall[at(p, 16, 8, offset), 128 * r : 128 * r + 128]
            t = [rows(r, 0) for r in range(R)]
            t += [jnp.where(upper, rows(2 * i, 8), rows(2 * i + 1, 8)) for i in range(3)]
            put(p, pack_lat(t))
        put.send(group)


def slot_rows(kc, eights, fours):
    if kc < 8:
        return eights, pl.ds(kc, H, stride=8)
    return fours, pl.ds(kc - 8, H, stride=4)


def height_ahead(froms, recv, eights, fours, wide, spec, fwd, fwd0):
    for group in froms:
        recv.wait(group)
        for p in group:
            t = unpack_lat(recv(p).astype(F32))
            eights[at(p, 48), :] = jnp.concatenate(t[:6], axis=0)
            fours[at(p, 24), :] = jnp.concatenate(t[6:], axis=0)
    for c in range(2):
        for k in range(KS):
            ref, rows = slot_rows(c * KS + k, eights, fours)
            wide[H * c : H * c + H, 128 * k : 128 * k + 128] = ref[rows, :]
    zero = table_dot(fwd0, wide[:, 0:128])
    rest = table_dot(fwd, wide[:, 128:])
    half = KS * H
    spec[0:H, 0:128] = zero[0:H]
    spec[0:H, 128:256] = zero[H : 2 * H]
    spec[half : half + H, 0:128] = zero[2 * H : 3 * H]
    spec[half : half + H, 128:256] = zero[3 * H :]
    for k in range(1, KS):
        real, imag = rest[0:H, 128 * (k - 1) : 128 * k], rest[H:, 128 * (k - 1) : 128 * k]
        spec[H * k : H * k + H, 0:128] = real
        spec[H * k : H * k + H, 128:256] = imag
        spec[half + H * k : half + H * k + H, 0:128] = real
        spec[half + H * k : half + H * k + H, 128:256] = -imag


def height_back(spec, eights, fours, wide, first, inv, inv0, tos, put):
    half = KS * H
    for i, (start, lane) in enumerate(((0, 0), (0, 128), (half, 0), (half, 128))):
        first[H * i : H * i + H, :] = spec[start : start + H, lane : lane + 128]
    for k in range(1, KS):
        low = spec[H * k : H * k + H, :]
        high = spec[half + H * k : half + H * k + H, :]
        wide[0:H, 128 * k : 128 * k + 128] = low[:, 0:128] + high[:, 0:128]
        wide[H : 2 * H, 128 * k : 128 * k + 128] = low[:, 128:] - high[:, 128:]
    zero = table_dot(inv0, first[...])
    rest = table_dot(inv, wide[:, 128:])
    for c in range(2):
        for k in range(KS):
            ref, rows = slot_rows(c * KS + k, eights, fours)
            values = zero[H * c : H * c + H] if k == 0 else rest[H * c : H * c + H, 128 * (k - 1) : 128 * k]
            ref[rows, :] = values
    for group in tos:
        for p in group:
            t = [eights[at(p, 48, 8, 8 * i), :] for i in range(6)]
            t += [fours[at(p, 24, 8, 8 * i), :] for i in range(3)]
            put(p, pack_lat(t))
        put.send(group)


def width_back(froms, recv, tall, wide, even, odd, tos, put):
    for group in froms:
        recv.wait(group)
        for p in group:
            t = unpack_lat(recv(p).astype(F32))
            for r in range(R):
                lane = 128 * (r // 2) + 384 * (r % 2)
                tall[at(p, 16, 8), lane : lane + 128] = t[r]
                tall[at(p, 16, 8, 8), lane : lane + 128] = t[6 + r // 2]
    wide[:, 0:384] = table_dot(even, tall[:, 0:384])
    wide[:, 384:768] = table_dot(odd, tall[:, 384:768])
    for group in tos:
        for j in group:
            m = [wide[at(j, C), 128 * (r // 2) + 384 * (r % 2) : 128 * (r // 2) + 384 * (r % 2) + 128] for r in range(R)]
            put(j, pack_lon(jnp.concatenate(m, axis=0)))
        put.send(group)


def gathered(recv):
    recv.wait(range(NJ))
    return joined_blocks([unpack_lon(recv(b).astype(F32))[:, 0:128] for b in range(NJ)])


def matrix_dot(values, matrix):
    return dot(values.astype(BF16), matrix[0])


def matrix_dot_nt(values, matrix):
    return dot_nt(values.astype(BF16), matrix[0])


CHUNK = 192


def spectral_ahead(loop, spec, first_pre, squares, mat1, bias1, mat2, bias2):
    def step(i):
        rows = pl.ds(pl.multiple_of(i * CHUNK, CHUNK), CHUNK)
        pre = matrix_dot(spec[rows, :], mat1) + bias1[...]
        first_pre[rows, :] = pre
        second = matrix_dot(pre * cumulative(pre), mat2) + bias2[...]
        slope = jnp.tanh(second * (1.0 / THRESHOLD))
        squares[rows, :] = slope * slope
        spec[rows, :] = second - THRESHOLD * slope
    loop(ROWS // CHUNK, step)


def spectral_slopes(loop, first_pre):
    def step(i):
        rows = pl.ds(pl.multiple_of(i * CHUNK, CHUNK), CHUNK)
        pre = first_pre[rows, :]
        first_pre[rows, :] = cumulative(pre) + pre * density(pre)
    loop(ROWS // CHUNK, step)


def spectral_adjoint(loop, spec, slopes, squares, mat1, mat2):
    def step(i):
        rows = pl.ds(pl.multiple_of(i * CHUNK, CHUNK), CHUNK)
        grad = matrix_dot_nt(spec[rows, :] * squares[rows, :], mat2)
        spec[rows, :] = matrix_dot_nt(grad * slopes[rows, :], mat1)
    loop(ROWS // CHUNK, step)


def fill_matrix(out, weight):
    out[...] = jnp.zeros_like(out)
    real, imag = weight[0, 0], weight[1, 0]
    out[0, 0:BS, 0:BS] = real.astype(BF16)
    out[0, 0:BS, 128 : 128 + BS] = imag.astype(BF16)
    out[0, 128 : 128 + BS, 0:BS] = (-imag).astype(BF16)
    out[0, 128 : 128 + BS, 128 : 128 + BS] = real.astype(BF16)


def fill_first(fwd0, inv0, fwd, inv, packed):
    left = lax.broadcasted_iota(jnp.int32, (1, 2 * H), 1) < H
    one = jnp.where(packed, 0.0, 1.0)
    first = jnp.where(left, 1.0, one)
    second = jnp.where(left, one, 1.0)
    for i in range(2):
        real, imag = fwd[i, 0:H].astype(F32), fwd[i, H : 2 * H].astype(F32)
        fwd0[i, 0:H] = (real * first).astype(BF16)
        fwd0[i, H : 2 * H] = (imag * first).astype(BF16)
        fwd0[i, 2 * H : 3 * H] = (jnp.where(packed, imag, real) * second).astype(BF16)
        fwd0[i, 3 * H : 4 * H] = (-jnp.where(packed, real, imag) * second).astype(BF16)
    real, imag = inv[0:H].astype(F32), inv[H : 2 * H].astype(F32)
    sign = jnp.where(left, 1.0, -1.0)
    inv0[0:H, 0 : 2 * H] = jnp.where(packed, 2.0 * real, real).astype(BF16)
    inv0[H : 2 * H, 0 : 2 * H] = (imag * one).astype(BF16)
    inv0[0:H, 2 * H : 4 * H] = (real * sign * one).astype(BF16)
    inv0[H : 2 * H, 2 * H : 4 * H] = jnp.where(packed, 2.0 * real, imag * sign).astype(BF16)


def fill_bias(out, bias):
    out[...] = jnp.zeros_like(out)
    out[0:1, 0:BS] = bias[0]
    out[0:1, 128 : 128 + BS] = bias[1]


def token_ahead(loop, mixed, cot, held, fc1, bias1, gain2, shift2, hidden, gh, acc):
    normed, inverse = layer_norm(mixed)
    v = (normed * gain2 + shift2).astype(BF16)
    acc[...] = jnp.zeros_like(acc)

    def step(n):
        cols = pl.ds(pl.multiple_of(n * HC, HC), HC)
        pre = dot(v, fc1[:, cols]) + bias1[cols].reshape(1, -1)
        phi = cumulative(pre)
        hidden[held, cols] = (pre * phi).astype(BF16)
        grad = (gh[held, cols] * (phi + pre * density(pre))).astype(BF16)
        acc[...] += dot_nt(grad, fc1[:, cols])
    loop(FF // HC, step)
    return (cot + norm_backward(acc[...], gain2, normed, inverse)).astype(BF16).astype(F32)


def kernel(
    *refs,
):
    sources, rest = refs[:19], refs[19:]
    (
        advanced, sensitivity,
        state, weight1, bias_1, weight2, bias_2, gain1, shift1, gain2, shift2, fc1, fc1_bias, fc2, fc2_bias, cotangent,
        ahead, fwd, even, odd, inv,
        lon_send, lon_recv, lat_send, lat_recv, lowered, mixed, grads, hidden, gh, acc,
        wide, tall, eights, fours, first, spec, first_pre, squares, mat1, mat2, bias1, bias2, fwd0, inv0,
        load_sem, lon_send_sem, lon_recv_sem, lat_send_sem, lat_recv_sem,
    ) = rest
    p = lax.axis_index("lat")
    j = lax.axis_index("lon")

    def loop(count, body):
        lax.fori_loop(0, count, lambda i, _: (body(i), 0)[1], 0)

    ens = lax.axis_index("ens")
    lon_ring = [(dx, dy) for dx in (2, 1, 3, 0) for dy in (0, 1)]
    lat_ring = [(dz, dc) for dz in (4, 3, 5, 2, 6, 1, 7, 0) for dc in (0, 1)]

    def lon_peers(sign):
        return [lax.rem(j // 2 + 4 + sign * dx, 4) * 2 + lax.rem(j + dy, 2) for dx, dy in lon_ring]

    def lat_peers(sign):
        return [lax.rem(p // 2 + 8 + sign * dz, 8) * 2 + lax.rem(p + dc, 2) for dz, dc in lat_ring if dz + dc]

    lon_to, lon_from, lat_to, lat_from = lon_peers(1), lon_peers(-1), lat_peers(1), lat_peers(-1)

    def device(axis, to):
        return {"lon": to, "ens": 1 - ens} if axis == "lon" else {"lat": to}

    barrier = pltpu.get_barrier_semaphore()
    for axis, peers in (("lat", lat_to), ("lon", lon_to)):
        for to in peers:
            pl.semaphore_signal(barrier, inc=1, device_id=device(axis, to), device_id_type=pl.DeviceIdType.MESH)
    held_here = (
        state, weight1, bias_1, weight2, bias_2, gain1, shift1, gain2, shift2, fc1, fc1_bias, fc2, fc2_bias, cotangent,
        ahead, fwd, even, odd, inv,
    )
    loads = [pltpu.make_async_copy(a, b, load_sem.at[i]) for i, (a, b) in enumerate(zip(sources, held_here))]
    for i in FIRST + MIDDLE + LAST:
        loads[i].start()
    for i in FIRST:
        loads[i].wait()

    def buffers(x, s, axis):
        e = 2 * x + s
        if axis == "lon":
            return lon_send, lon_recv, lon_send_sem, lon_recv_sem, e, j
        return lat_send, lat_recv, lat_send_sem, lat_recv_sem, e, p

    def copy(x, s, axis, to, slot):
        send, recv, send_sem, recv_sem, e, me = buffers(x, s, axis)
        return pltpu.make_async_remote_copy(
            src_ref=send.at[e, to],
            dst_ref=recv.at[e, slot],
            send_sem=send_sem.at[e],
            recv_sem=recv_sem.at[e, slot],
            device_id=device(axis, to),
            device_id_type=pl.DeviceIdType.MESH,
        )

    class Sender:
        def __init__(self, x, s, axis):
            self.where = (x, s, axis)

        def __call__(self, to, values):
            send, recv, _, _, e, _ = buffers(*self.where)
            (recv if to is p else send)[e, to] = values.astype(BF16)

        def send(self, group):
            me = buffers(*self.where)[-1]
            for to in group:
                if to is not p:
                    copy(*self.where, to, me).start()

    class Receiver:
        def __init__(self, x, s, axis):
            self.where = (x, s, axis)

        def wait(self, group):
            for source in group:
                if source is not p:
                    copy(*self.where, source, source).wait_recv()

        def __call__(self, source):
            _, recv, _, _, e, _ = buffers(*self.where)
            return recv[e, source]

    sender, receiver = Sender, Receiver

    def halves(peers):
        return [peers[: len(peers) // 2], peers[len(peers) // 2 :]]

    def sent(x, s, axis, count):
        send, recv, send_sem, recv_sem, e, me = buffers(x, s, axis)
        pltpu.make_async_remote_copy(
            src_ref=send.at[e, pl.ds(0, count)],
            dst_ref=recv.at[e, pl.ds(0, count)],
            send_sem=send_sem.at[e],
            recv_sem=recv_sem.at[e, 0],
            device_id=device(axis, lon_to[0] if axis == "lon" else lat_to[0]),
            device_id_type=pl.DeviceIdType.MESH,
        ).wait_send()

    def tokens(ref, s):
        return jnp.concatenate([ref[s, r].astype(F32) for r in range(R)], axis=0)

    def out_tokens(ref, s, values):
        for r in range(R):
            ref[s, r] = values[C * r : C * r + C].astype(BF16)

    def held(s):
        return pl.ds(TOK * s, TOK)

    def send_tokens(x, s, ref):
        e = 2 * x + s
        for b in range(NJ):
            lon_send[e, b] = pack_lon(feature_block(lambda t: ref[s, :, 128 * t : 128 * t + 128], b)).astype(BF16)
        if e == 0:
            pl.semaphore_wait(barrier, NP - 1 + NJ)
        for to in lon_to:
            copy(x, s, "lon", to, j).start()

    for s in range(2):
        with jax.named_scope("ln"):
            normed, _ = layer_norm(tokens(state, s))
            lowered[s] = (normed * row(gain1) + row(shift1)).astype(BF16).astype(F32)
            send_tokens(0, s, lowered)
    for i in MIDDLE:
        loads[i].wait()
    fill_matrix(mat1, weight1)
    fill_matrix(mat2, weight2)
    fill_bias(bias1, bias_1)
    fill_bias(bias2, bias_2)
    fill_first(fwd0, inv0, fwd, inv, p == 0)

    for s in range(2):
        with jax.named_scope("w0"):
            width_ahead(halves(lon_from), receiver(0, s, "lon"), wide, tall, ahead, halves(lat_to + [p]), sender(0, s, "lat"))

    with jax.named_scope("gh"):
        loads[11].wait()
        cots = jnp.concatenate([tokens(cotangent, s) for s in range(2)], axis=0).astype(BF16)

        def cot_step(n):
            cols = pl.ds(pl.multiple_of(n * HC, HC), HC)
            gh[:, cols] = dot_nt(cots, fc2[cols, :])
        loop(FF // HC, cot_step)

    for s in range(2):
        with jax.named_scope("h0"):
            height_ahead(halves([p] + lat_from), receiver(0, s, "lat"), eights, fours, wide, spec, fwd, fwd0)
        with jax.named_scope("sp0"):
            spectral_ahead(loop, spec, first_pre.at[s], squares.at[s], mat1, bias1, mat2, bias2)
        with jax.named_scope("hb1"):
            height_back(spec, eights, fours, wide, first, inv, inv0, halves(lat_to + [p]), sender(1, s, "lat"))
    for s in range(2):
        with jax.named_scope("slopes"):
            spectral_slopes(loop, first_pre.at[s])
    loads[9].wait()
    for s in range(2):
        with jax.named_scope("wb1"):
            width_back(halves([p] + lat_from), receiver(1, s, "lat"), tall, wide, even, odd, halves(lon_to), sender(1, s, "lon"))
    for s in range(2):
        with jax.named_scope("gath1"):
            filtered = gathered(receiver(1, s, "lon"))
            mixed[s] = (filtered + lowered[s] + tokens(state, s)).astype(BF16).astype(F32)
        with jax.named_scope("token"):
            grads[s] = token_ahead(
                loop, mixed[s], tokens(cotangent, s), held(s), fc1, fc1_bias, row(gain2), row(shift2), hidden, gh, acc
            )
        with jax.named_scope("sendt"):
            send_tokens(2, s, grads)

    def advance(s):
        for n in range(D // 256):
            cols = slice(256 * n, 256 * n + 256)
            values = dot(hidden[TOK * s : TOK * s + TOK, :], fc2[:, cols]) + fc2_bias[cols].reshape(1, -1) + mixed[s, :, cols]
            for r in range(R):
                advanced[s, r, :, cols] = values[C * r : C * r + C].astype(BF16)

    for s in range(2):
        with jax.named_scope("w2"):
            width_ahead(halves(lon_from), receiver(2, s, "lon"), wide, tall, ahead, halves(lat_to + [p]), sender(2, s, "lat"))
    for s in range(2):
        with jax.named_scope("adv"):
            advance(s)
    for s in range(2):
        with jax.named_scope("h2"):
            height_ahead(halves([p] + lat_from), receiver(2, s, "lat"), eights, fours, wide, spec, fwd, fwd0)
        with jax.named_scope("sp2"):
            spectral_adjoint(loop, spec, first_pre.at[s], squares.at[s], mat1, mat2)
        with jax.named_scope("hb3"):
            height_back(spec, eights, fours, wide, first, inv, inv0, halves(lat_to + [p]), sender(3, s, "lat"))
    for s in range(2):
        with jax.named_scope("wb3"):
            width_back(halves([p] + lat_from), receiver(3, s, "lat"), tall, wide, even, odd, halves(lon_to), sender(3, s, "lon"))
    for s in range(2):
        with jax.named_scope("final"):
            grad = grads[s]
            grad_lowered = gathered(receiver(3, s, "lon")) + grad
            normed, inverse = layer_norm(tokens(state, s))
            out_tokens(sensitivity, s, grad + norm_backward(grad_lowered, row(gain1), normed, inverse))
    for x in range(4):
        for s in range(2):
            sent(x, s, "lon", NJ)
            sent(x, s, "lat", NP - 1)


def finish(advanced, sensitivity, advanced_out, sensitivity_out):
    advanced_out[...] = advanced[...]
    sensitivity_out[...] = sensitivity[...]


def shards(
    state, spec_weight1, spec_bias1, spec_weight2, spec_bias2, norm1_gain, norm1_bias, norm2_gain, norm2_bias,
    fc1_weight, fc1_bias, fc2_weight, fc2_bias, cotangent,
):
    vmem = pl.BlockSpec(memory_space=pltpu.VMEM)
    hbm = pl.BlockSpec(memory_space=pltpu.HBM)
    names = [jnp.asarray(t) for t in tables()]
    operands = [
        state, spec_weight1, spec_bias1, spec_weight2, spec_bias2, norm1_gain, norm1_bias, norm2_gain,
        norm2_bias, fc1_weight, fc1_bias, fc2_weight, fc2_bias, cotangent, *names,
    ]
    specs = [hbm] * len(operands)
    out = jax.ShapeDtypeStruct(state.shape, BF16)
    results = pl.pallas_call(
        kernel,
        out_shape=(out, out),
        in_specs=specs,
        out_specs=(vmem, vmem),
        scratch_shapes=[
            *[pltpu.VMEM(a.shape, a.dtype) for a in operands],
            pltpu.VMEM((8, NJ, 112, 128), BF16),
            pltpu.VMEM((8, NJ, 112, 128), BF16),
            pltpu.VMEM((8, NP, 56, 128), BF16),
            pltpu.VMEM((8, NP, 56, 128), BF16),
            pltpu.VMEM((2, TOK, D), F32),
            pltpu.VMEM((2, TOK, D), F32),
            pltpu.VMEM((2, TOK, D), F32),
            pltpu.VMEM((2 * TOK, FF), BF16),
            pltpu.VMEM((2 * TOK, FF), F32),
            pltpu.VMEM((TOK, D), F32),
            pltpu.VMEM((W, D), F32),
            pltpu.VMEM((16 * NP, D), F32),
            pltpu.VMEM((8 * H, 128), F32),
            pltpu.VMEM((4 * H, 128), F32),
            pltpu.VMEM((4 * H, 128), F32),
            pltpu.VMEM((ROWS, 256), F32),
            pltpu.VMEM((2, ROWS, 256), F32),
            pltpu.VMEM((2, ROWS, 256), F32),
            pltpu.VMEM((1, 256, 256), BF16),
            pltpu.VMEM((1, 256, 256), BF16),
            pltpu.VMEM((1, 256), F32),
            pltpu.VMEM((1, 256), F32),
            pltpu.VMEM((2, 4 * H, 2 * H), BF16),
            pltpu.VMEM((2 * H, 4 * H), BF16),
            pltpu.SemaphoreType.DMA((len(operands),)),
            pltpu.SemaphoreType.DMA((8,)),
            pltpu.SemaphoreType.DMA((8, NJ)),
            pltpu.SemaphoreType.DMA((8,)),
            pltpu.SemaphoreType.DMA((8, NP)),
        ],
        compiler_params=pltpu.CompilerParams(
            collective_id=0, has_side_effects=True, vmem_limit_bytes=67043328
        ),
        name="block",
    )(*operands)
    return pl.pallas_call(
        finish,
        out_shape=(out, out),
        in_specs=[vmem, vmem],
        out_specs=(vmem, vmem),
        compiler_params=pltpu.CompilerParams(vmem_limit_bytes=67043328),
        name="finish",
    )(*results)


def solution(mesh):
    in_specs = (
        P("ens", "lat", "lon", None),
        P(None, "lon", None, None),
        P(None, "lon", None),
        P(None, "lon", None, None),
        P(None, "lon", None),
        P(), P(), P(), P(), P(), P(), P(), P(),
        P("ens", "lat", "lon", None),
    )
    out_specs = (P("ens", "lat", "lon", None), P("ens", "lat", "lon", None))
    return jax.shard_map(shards, mesh=mesh, in_specs=in_specs, out_specs=out_specs, check_vma=False)
```

time: 100 us -> 90.5 us (0.905)
  local copies, waits for them, and re-layouts: 9.97 us -> 0 us
    reshape x5 -> x0, local copies, waits for them, and re-layouts: 6.36 us -> none  [shards(): row = lambda a: a.reshape(1, -1)]
    unnamed x2 -> x0, local copies, waits for them, and re-layouts: 3.61 us -> none
    pallas_call x0 -> x1, Pallas kernels: none -> 2.08 us  [shards(): pl.pallas_call(finish, out_shape=(out, out), in_specs=[vmem, vmem], out_s...]
    pallas_call x1, Pallas kernels: 89.5 us -> 87.7 us  [shards(): pl.pallas_call(kernel, out_shape=(out, out), in_specs=specs, out_specs=(v...]
where the time goes in v1:
time: 90.5 us; the launch traced here: 90.4 us
  Pallas kernels  89.8 us (99%)
    pallas_call x1, Pallas kernels, shards(): pl.pallas_call(kernel, out_shape=(out, out), in_specs=specs, out_specs=(v...  87.7 us
    pallas_call x1, Pallas kernels, shards(): pl.pallas_call(finish, out_shape=(out, out), in_specs=[vmem, vmem], out_s...  2.08 us

profile of v1, /device:TPU:1, one launch (start us, length us, event | category | flops | bytes accessed | tf_op | source)
XLA Modules:
  0.0 90.4 jit_solution(17587579564869150318)
XLA Ops:
  0.6 87.7 %block.1 = (bf16[2,6,24,768]{3,2,1,0:T(8,128)(2,1)}, bf16[2,6,24,768]{3,2,1,0:T(8,128)(2,1)}) custom-call(bf16[2,6,24,768]{3,2,1,0:T(8,128)(2,1)} %refs_0_.1, f32[2,1,96,96]{3,2,1,0:T(8,128)} %refs_1_.1, f32[2,1,96]{2,1,0:T(1,128)} %refs_2_.1, f32[2,1,96,96]{3,2,1,0:T(8,128)} %refs_3_.1, f32[2,1,96]{2,1,0:T(1,128)} %refs_4_.1, f32[768]{0:T(1024)} %refs_5_.1, ...), custom_call_target="tpu_custom_call" | custom-call | tf_op jit(solution)/shard_map/block/pallas_call | solution.py:605
  88.3 2.1 %finish.1 = (bf16[2,6,24,768]{3,2,1,0:T(8,128)(2,1)}, bf16[2,6,24,768]{3,2,1,0:T(8,128)(2,1)}) custom-call(bf16[2,6,24,768]{3,2,1,0:T(8,128)(2,1)} %get-tuple-element.4.advanced, bf16[2,6,24,768]{3,2,1,0:T(8,128)(2,1)} %get-tuple-element.5.sensitivity), custom_call_target="tpu_custom_call" | custom-call | tf_op jit(solution)/shard_map/finish/pallas_call | solution.py:647

commit v2 on v1

--- a/solution.py
+++ b/solution.py
@@ -279,7 +279,8 @@
 
 
 def gathered(recv):
-    recv.wait(range(NJ))
+    recv.wait(range(NJ // 2))
+    recv.wait(range(NJ // 2))
     return joined_blocks([unpack_lon(recv(b).astype(F32))[:, 0:128] for b in range(NJ)])
 
 
@@ -287,39 +288,32 @@
     return dot(values.astype(BF16), matrix[0])
 
 
-def matrix_dot_nt(values, matrix):
-    return dot_nt(values.astype(BF16), matrix[0])
-
-
-CHUNK = 192
-
-
-def spectral_ahead(loop, spec, first_pre, squares, mat1, bias1, mat2, bias2):
-    def step(i):
-        rows = pl.ds(pl.multiple_of(i * CHUNK, CHUNK), CHUNK)
+CHUNK = 384
+
+
+def spectral_ahead(spec, first_pre, squares, mat1, bias1, mat2, bias2):
+    for i in range(ROWS // CHUNK):
+        rows = slice(i * CHUNK, i * CHUNK + CHUNK)
         pre = matrix_dot(spec[rows, :], mat1) + bias1[...]
         first_pre[rows, :] = pre
         second = matrix_dot(pre * cumulative(pre), mat2) + bias2[...]
         slope = jnp.tanh(second * (1.0 / THRESHOLD))
         squares[rows, :] = slope * slope
         spec[rows, :] = second - THRESHOLD * slope
-    loop(ROWS // CHUNK, step)
-
-
-def spectral_slopes(loop, first_pre):
-    def step(i):
-        rows = pl.ds(pl.multiple_of(i * CHUNK, CHUNK), CHUNK)
+
+
+def spectral_slopes(first_pre):
+    for i in range(ROWS // CHUNK):
+        rows = slice(i * CHUNK, i * CHUNK + CHUNK)
         pre = first_pre[rows, :]
         first_pre[rows, :] = cumulative(pre) + pre * density(pre)
-    loop(ROWS // CHUNK, step)
-
-
-def spectral_adjoint(loop, spec, slopes, squares, mat1, mat2):
-    def step(i):
-        rows = pl.ds(pl.multiple_of(i * CHUNK, CHUNK), CHUNK)
-        grad = matrix_dot_nt(spec[rows, :] * squares[rows, :], mat2)
-        spec[rows, :] = matrix_dot_nt(grad * slopes[rows, :], mat1)
-    loop(ROWS // CHUNK, step)
+
+
+def spectral_adjoint(spec, slopes, squares, mat1, mat2):
+    for i in range(ROWS // CHUNK):
+        rows = slice(i * CHUNK, i * CHUNK + CHUNK)
+        grad = matrix_dot(spec[rows, :] * squares[rows, :], mat2)
+        spec[rows, :] = matrix_dot(grad * slopes[rows, :], mat1)
 
 
 def fill_matrix(out, weight):
@@ -350,6 +344,12 @@
     inv0[H : 2 * H, 2 * H : 4 * H] = jnp.where(packed, 2.0 * real, imag * sign).astype(BF16)
 
 
+def fill_transposed(out, matrix):
+    n = out.shape[-1]
+    one = lax.broadcasted_iota(jnp.int32, (n, n), 0) == lax.broadcasted_iota(jnp.int32, (n, n), 1)
+    out[0] = dot_nt(jnp.where(one, 1.0, 0.0).astype(BF16), matrix[0]).astype(BF16)
+
+
 def fill_bias(out, bias):
     out[...] = jnp.zeros_like(out)
     out[0:1, 0:BS] = bias[0]
@@ -359,16 +359,16 @@
 def token_ahead(loop, mixed, cot, held, fc1, bias1, gain2, shift2, hidden, gh, acc):
     normed, inverse = layer_norm(mixed)
     v = (normed * gain2 + shift2).astype(BF16)
-    acc[...] = jnp.zeros_like(acc)
-
-    def step(n):
-        cols = pl.ds(pl.multiple_of(n * HC, HC), HC)
+    for n in range(FF // HC):
+        cols = slice(n * HC, n * HC + HC)
         pre = dot(v, fc1[:, cols]) + bias1[cols].reshape(1, -1)
         phi = cumulative(pre)
         hidden[held, cols] = (pre * phi).astype(BF16)
         grad = (gh[held, cols] * (phi + pre * density(pre))).astype(BF16)
-        acc[...] += dot_nt(grad, fc1[:, cols])
-    loop(FF // HC, step)
+        if n:
+            acc[...] += dot_nt(grad, fc1[:, cols])
+        else:
+            acc[...] = dot_nt(grad, fc1[:, cols])
     return (cot + norm_backward(acc[...], gain2, normed, inverse)).astype(BF16).astype(F32)
 
 
@@ -377,12 +377,12 @@
 ):
     sources, rest = refs[:19], refs[19:]
     (
-        advanced, sensitivity,
-        state, weight1, bias_1, weight2, bias_2, gain1, shift1, gain2, shift2, fc1, fc1_bias, fc2, fc2_bias, cotangent,
+        advanced_hbm, sensitivity_hbm,
+        advanced, sensitivity, state, weight1, bias_1, weight2, bias_2, gain1, shift1, gain2, shift2, fc1, fc1_bias, fc2, fc2_bias, cotangent,
         ahead, fwd, even, odd, inv,
         lon_send, lon_recv, lat_send, lat_recv, lowered, mixed, grads, hidden, gh, acc,
-        wide, tall, eights, fours, first, spec, first_pre, squares, mat1, mat2, bias1, bias2, fwd0, inv0,
-        load_sem, lon_send_sem, lon_recv_sem, lat_send_sem, lat_recv_sem,
+        wide, tall, eights, fours, first, spec, first_pre, squares, mat1, mat2, turned1, turned2, bias1, bias2, fwd0, inv0,
+        load_sem, store_sem, lon_send_sem, lon_recv_sem, lat_send_sem, lat_recv_sem,
     ) = rest
     p = lax.axis_index("lat")
     j = lax.axis_index("lon")
@@ -425,59 +425,57 @@
             return lon_send, lon_recv, lon_send_sem, lon_recv_sem, e, j
         return lat_send, lat_recv, lat_send_sem, lat_recv_sem, e, p
 
-    def copy(x, s, axis, to, slot):
+    def copy(x, s, axis, to, half):
         send, recv, send_sem, recv_sem, e, me = buffers(x, s, axis)
         return pltpu.make_async_remote_copy(
             src_ref=send.at[e, to],
-            dst_ref=recv.at[e, slot],
+            dst_ref=recv.at[e, me],
             send_sem=send_sem.at[e],
-            recv_sem=recv_sem.at[e, slot],
+            recv_sem=recv_sem.at[e, half],
             device_id=device(axis, to),
             device_id_type=pl.DeviceIdType.MESH,
         )
 
+    def several(x, s, axis, count, half):
+        send, recv, send_sem, recv_sem, e, me = buffers(x, s, axis)
+        return pltpu.make_async_remote_copy(
+            src_ref=send.at[e, pl.ds(0, count)],
+            dst_ref=recv.at[e, pl.ds(0, count)],
+            send_sem=send_sem.at[e],
+            recv_sem=recv_sem.at[e, half],
+            device_id=device(axis, lon_to[0] if axis == "lon" else lat_to[0]),
+            device_id_type=pl.DeviceIdType.MESH,
+        )
+
     class Sender:
         def __init__(self, x, s, axis):
-            self.where = (x, s, axis)
+            self.where, self.half = (x, s, axis), 0
 
         def __call__(self, to, values):
             send, recv, _, _, e, _ = buffers(*self.where)
             (recv if to is p else send)[e, to] = values.astype(BF16)
 
         def send(self, group):
-            me = buffers(*self.where)[-1]
             for to in group:
                 if to is not p:
-                    copy(*self.where, to, me).start()
+                    copy(*self.where, to, self.half).start()
+            self.half += 1
 
     class Receiver:
         def __init__(self, x, s, axis):
-            self.where = (x, s, axis)
+            self.where, self.half = (x, s, axis), 0
 
         def wait(self, group):
-            for source in group:
-                if source is not p:
-                    copy(*self.where, source, source).wait_recv()
+            several(*self.where, len([0 for source in group if source is not p]), self.half).wait_recv()
+            self.half += 1
 
         def __call__(self, source):
             _, recv, _, _, e, _ = buffers(*self.where)
             return recv[e, source]
 
     sender, receiver = Sender, Receiver
-
-    def halves(peers):
-        return [peers[: len(peers) // 2], peers[len(peers) // 2 :]]
-
-    def sent(x, s, axis, count):
-        send, recv, send_sem, recv_sem, e, me = buffers(x, s, axis)
-        pltpu.make_async_remote_copy(
-            src_ref=send.at[e, pl.ds(0, count)],
-            dst_ref=recv.at[e, pl.ds(0, count)],
-            send_sem=send_sem.at[e],
-            recv_sem=recv_sem.at[e, 0],
-            device_id=device(axis, lon_to[0] if axis == "lon" else lat_to[0]),
-            device_id_type=pl.DeviceIdType.MESH,
-        ).wait_send()
+    lon_tos, lon_froms = [lon_to[:4], lon_to[4:]], [lon_from[:4], lon_from[4:]]
+    lat_tos, lat_froms = [lat_to[:8], lat_to[8:] + [p]], [[p] + lat_from[:8], lat_from[8:]]
 
     def tokens(ref, s):
         return jnp.concatenate([ref[s, r].astype(F32) for r in range(R)], axis=0)
@@ -487,7 +485,7 @@
             ref[s, r] = values[C * r : C * r + C].astype(BF16)
 
     def held(s):
-        return pl.ds(TOK * s, TOK)
+        return slice(TOK * s, TOK * s + TOK)
 
     def send_tokens(x, s, ref):
         e = 2 * x + s
@@ -495,8 +493,9 @@
             lon_send[e, b] = pack_lon(feature_block(lambda t: ref[s, :, 128 * t : 128 * t + 128], b)).astype(BF16)
         if e == 0:
             pl.semaphore_wait(barrier, NP - 1 + NJ)
-        for to in lon_to:
-            copy(x, s, "lon", to, j).start()
+        for half in range(2):
+            for to in lon_tos[half]:
+                copy(x, s, "lon", to, half).start()
 
     for s in range(2):
         with jax.named_scope("ln"):
@@ -507,13 +506,15 @@
         loads[i].wait()
     fill_matrix(mat1, weight1)
     fill_matrix(mat2, weight2)
+    fill_transposed(turned1, mat1)
+    fill_transposed(turned2, mat2)
     fill_bias(bias1, bias_1)
     fill_bias(bias2, bias_2)
     fill_first(fwd0, inv0, fwd, inv, p == 0)
 
     for s in range(2):
         with jax.named_scope("w0"):
-            width_ahead(halves(lon_from), receiver(0, s, "lon"), wide, tall, ahead, halves(lat_to + [p]), sender(0, s, "lat"))
+            width_ahead(lon_froms, receiver(0, s, "lon"), wide, tall, ahead, lat_tos, sender(0, s, "lat"))
 
     with jax.named_scope("gh"):
         loads[11].wait()
@@ -526,18 +527,18 @@
 
     for s in range(2):
         with jax.named_scope("h0"):
-            height_ahead(halves([p] + lat_from), receiver(0, s, "lat"), eights, fours, wide, spec, fwd, fwd0)
+            height_ahead(lat_froms, receiver(0, s, "lat"), eights, fours, wide, spec, fwd, fwd0)
         with jax.named_scope("sp0"):
-            spectral_ahead(loop, spec, first_pre.at[s], squares.at[s], mat1, bias1, mat2, bias2)
+            spectral_ahead(spec, first_pre.at[s], squares.at[s], mat1, bias1, mat2, bias2)
         with jax.named_scope("hb1"):
-            height_back(spec, eights, fours, wide, first, inv, inv0, halves(lat_to + [p]), sender(1, s, "lat"))
+            height_back(spec, eights, fours, wide, first, inv, inv0, lat_tos, sender(1, s, "lat"))
     for s in range(2):
         with jax.named_scope("slopes"):
-            spectral_slopes(loop, first_pre.at[s])
+            spectral_slopes(first_pre.at[s])
     loads[9].wait()
     for s in range(2):
         with jax.named_scope("wb1"):
-            width_back(halves([p] + lat_from), receiver(1, s, "lat"), tall, wide, even, odd, halves(lon_to), sender(1, s, "lon"))
+            width_back(lat_froms, receiver(1, s, "lat"), tall, wide, even, odd, lon_tos, sender(1, s, "lon"))
     for s in range(2):
         with jax.named_scope("gath1"):
             filtered = gathered(receiver(1, s, "lon"))
@@ -549,6 +550,10 @@
         with jax.named_scope("sendt"):
             send_tokens(2, s, grads)
 
+    def store(i, s):
+        source, target = ((advanced, advanced_hbm), (sensitivity, sensitivity_hbm))[i]
+        return pltpu.make_async_copy(source.at[s], target.at[s], store_sem.at[2 * i + s])
+
     def advance(s):
         for n in range(D // 256):
             cols = slice(256 * n, 256 * n + 256)
@@ -558,30 +563,37 @@
 
     for s in range(2):
         with jax.named_scope("w2"):
-            width_ahead(halves(lon_from), receiver(2, s, "lon"), wide, tall, ahead, halves(lat_to + [p]), sender(2, s, "lat"))
+            width_ahead(lon_froms, receiver(2, s, "lon"), wide, tall, ahead, lat_tos, sender(2, s, "lat"))
     for s in range(2):
         with jax.named_scope("adv"):
             advance(s)
+        store(0, s).start()
     for s in range(2):
         with jax.named_scope("h2"):
-            height_ahead(halves([p] + lat_from), receiver(2, s, "lat"), eights, fours, wide, spec, fwd, fwd0)
+            height_ahead(lat_froms, receiver(2, s, "lat"), eights, fours, wide, spec, fwd, fwd0)
         with jax.named_scope("sp2"):
-            spectral_adjoint(loop, spec, first_pre.at[s], squares.at[s], mat1, mat2)
+            spectral_adjoint(spec, first_pre.at[s], squares.at[s], turned1, turned2)
         with jax.named_scope("hb3"):
-            height_back(spec, eights, fours, wide, first, inv, inv0, halves(lat_to + [p]), sender(3, s, "lat"))
+            height_back(spec, eights, fours, wide, first, inv, inv0, lat_tos, sender(3, s, "lat"))
     for s in range(2):
         with jax.named_scope("wb3"):
-            width_back(halves([p] + lat_from), receiver(3, s, "lat"), tall, wide, even, odd, halves(lon_to), sender(3, s, "lon"))
+            width_back(lat_froms, receiver(3, s, "lat"), tall, wide, even, odd, lon_tos, sender(3, s, "lon"))
     for s in range(2):
         with jax.named_scope("final"):
             grad = grads[s]
             grad_lowered = gathered(receiver(3, s, "lon")) + grad
             normed, inverse = layer_norm(tokens(state, s))
             out_tokens(sensitivity, s, grad + norm_backward(grad_lowered, row(gain1), normed, inverse))
-    for x in range(4):
-        for s in range(2):
-            sent(x, s, "lon", NJ)
-            sent(x, s, "lat", NP - 1)
+        store(1, s).start()
+    with jax.named_scope("tail_sent"):
+        for x in range(4):
+            for s in range(2):
+                several(x, s, "lon", NJ, 0).wait_send()
+                several(x, s, "lat", NP - 1, 0).wait_send()
+    with jax.named_scope("tail_store"):
+        for i in range(2):
+            for s in range(2):
+                store(i, s).wait()
 
 
 def finish(advanced, sensitivity, advanced_out, sensitivity_out):
@@ -606,8 +618,10 @@
         kernel,
         out_shape=(out, out),
         in_specs=specs,
-        out_specs=(vmem, vmem),
+        out_specs=(hbm, hbm),
         scratch_shapes=[
+            pltpu.VMEM(state.shape, BF16),
+            pltpu.VMEM(state.shape, BF16),
             *[pltpu.VMEM(a.shape, a.dtype) for a in operands],
             pltpu.VMEM((8, NJ, 112, 128), BF16),
             pltpu.VMEM((8, NJ, 112, 128), BF16),
@@ -629,15 +643,18 @@
             pltpu.VMEM((2, ROWS, 256), F32),
             pltpu.VMEM((1, 256, 256), BF16),
             pltpu.VMEM((1, 256, 256), BF16),
+            pltpu.VMEM((1, 256, 256), BF16),
+            pltpu.VMEM((1, 256, 256), BF16),
             pltpu.VMEM((1, 256), F32),
             pltpu.VMEM((1, 256), F32),
             pltpu.VMEM((2, 4 * H, 2 * H), BF16),
             pltpu.VMEM((2 * H, 4 * H), BF16),
             pltpu.SemaphoreType.DMA((len(operands),)),
+            pltpu.SemaphoreType.DMA((4,)),
             pltpu.SemaphoreType.DMA((8,)),
-            pltpu.SemaphoreType.DMA((8, NJ)),
+            pltpu.SemaphoreType.DMA((8, 2)),
             pltpu.SemaphoreType.DMA((8,)),
-            pltpu.SemaphoreType.DMA((8, NP)),
+            pltpu.SemaphoreType.DMA((8, 2)),
         ],
         compiler_params=pltpu.CompilerParams(
             collective_id=0, has_side_effects=True, vmem_limit_bytes=67043328

time: 90.5 us -> 83 us (0.917)
  Pallas kernels: 89.8 us -> 82.2 us
    pallas_call x1, Pallas kernels: 87.7 us -> 80.2 us  [shards(): pl.pallas_call(kernel, out_shape=(out, out), in_specs=specs, out_specs=(h...]
where the time goes in v2:
time: 83 us; the launch traced here: 82.9 us
  Pallas kernels  82.2 us (99%)
    pallas_call x1, Pallas kernels, shards(): pl.pallas_call(kernel, out_shape=(out, out), in_specs=specs, out_specs=(h...  80.2 us
    pallas_call x1, Pallas kernels, shards(): pl.pallas_call(finish, out_shape=(out, out), in_specs=[vmem, vmem], out_s...  2.08 us

profile of v2, /device:TPU:1, one launch (start us, length us, event | category | flops | bytes accessed | tf_op | source)
XLA Modules:
  0.0 82.9 jit_solution(3873843097429859369)
XLA Ops:
  0.6 80.2 %block.1 = (bf16[2,6,24,768]{3,2,1,0:T(8,128)(2,1)}, bf16[2,6,24,768]{3,2,1,0:T(8,128)(2,1)}) custom-call(bf16[2,6,24,768]{3,2,1,0:T(8,128)(2,1)} %refs_0_.1, f32[2,1,96,96]{3,2,1,0:T(8,128)} %refs_1_.1, f32[2,1,96]{2,1,0:T(1,128)} %refs_2_.1, f32[2,1,96,96]{3,2,1,0:T(8,128)} %refs_3_.1, f32[2,1,96]{2,1,0:T(1,128)} %refs_4_.1, f32[768]{0:T(1024)} %refs_5_.1, ...), custom_call_target="tpu_custom_call" | custom-call | tf_op jit(solution)/shard_map/block/pallas_call | solution.py:617
  80.8 2.1 %finish.1 = (bf16[2,6,24,768]{3,2,1,0:T(8,128)(2,1)}, bf16[2,6,24,768]{3,2,1,0:T(8,128)(2,1)}) custom-call(bf16[2,6,24,768]{3,2,1,0:T(8,128)(2,1)} %get-tuple-element.4.advanced, bf16[2,6,24,768]{3,2,1,0:T(8,128)(2,1)} %get-tuple-element.5.sensitivity), custom_call_target="tpu_custom_call" | custom-call | tf_op jit(solution)/shard_map/finish/pallas_call | solution.py:664

commit v3 on v2

--- a/solution.py
+++ b/solution.py
@@ -26,7 +26,7 @@
 FF = 3072
 HC = 512
 ROWS = 2 * KS * H
-FIRST, MIDDLE, LAST = [0, 5, 6], [1, 2, 3, 4, 7, 8, 10, 12, 13, 14, 15, 16, 17, 18], [11, 9]
+FIRST, MIDDLE, LAST = [5, 6], [1, 2, 3, 4, 7, 8, 10, 12, 13, 14, 15, 16, 17, 18], [11, 9]
 
 roll = pltpu.roll
 
@@ -44,7 +44,7 @@
     odd = np.zeros((W, NP, 16))
     for p in range(NP):
         for kc in range(12):
-            c, k = divmod(kc, KS)
+            c, k = divmod(kc, 4) if kc < 8 else ((kc - 8) // 2, 4 + kc % 2)
             f = p * KS + k
             if c == 0:
                 row, back = cosine[:, f], (2.0 if f else 1.0) * cosine[:, f]
@@ -163,22 +163,42 @@
     return jnp.concatenate([m, extra], axis=0)
 
 
-def pack_lat(t):
+def beside(tile, extra, i):
+    return jnp.where(lanes() < 96, tile, roll(extra, 96 - 32 * i, 1))
+
+
+def from_beside(a, b, c):
     lane = lanes()
-    out = []
-    for i in range(R):
-        shift = 96 - 32 * (i % 3)
-        out.append(jnp.where(lane < 96, t[i], roll(t[7 + i // 3], shift, 1)))
-    return jnp.concatenate(out + [t[6]], axis=0)
-
-
-def unpack_lat(m):
-    lane = lanes()
-    t = [m[8 * i : 8 * i + 8] for i in range(7)]
-    for e in range(2):
-        a, b, c = t[3 * e : 3 * e + 3]
-        t.append(jnp.where(lane < 32, roll(a, 32, 1), jnp.where(lane < 64, roll(b, 64, 1), roll(c, 96, 1))))
-    return t
+    return jnp.where(lane < 32, roll(a, 32, 1), jnp.where(lane < 64, roll(b, 64, 1), roll(c, 96, 1)))
+
+
+OUT, BACK = 40, 32
+
+
+def pack_out(part, a, c):
+    if part == 0:
+        tiles = [beside(a[i], a[5], i) for i in range(3)] + [beside(a[3], c[2], 0), beside(a[4], c[2], 1)]
+    else:
+        tiles = [beside(c[0], c[2], 2), c[1]]
+    return jnp.concatenate(tiles, axis=0)
+
+
+def unpack_out(part, t):
+    if part == 0:
+        return t[:5] + [from_beside(*t[:3])]
+    return [t[5], t[6], from_beside(t[3], t[4], t[5])]
+
+
+def pack_back(part, a, c):
+    if part == 0:
+        tiles = [beside(a[i], a[4], i) for i in range(3)] + [beside(a[3], a[5], 0)]
+    else:
+        tiles = [beside(c[0], a[5], 1), beside(c[1], a[5], 2), c[2]]
+    return jnp.concatenate(tiles, axis=0)
+
+
+def eight_rows(m):
+    return [m[8 * i : 8 * i + 8] for i in range(m.shape[0] // 8)]
 
 
 def at(index, size, count=None, offset=0):
@@ -186,101 +206,128 @@
 
 
 def width_ahead(froms, recv, wide, tall, ahead, tos, put):
-    for group in froms:
-        recv.wait(group)
+    for half, group in enumerate(froms):
+        recv.wait(len(group), 0, 112, half)
         for j in group:
             m = unpack_lon(recv(j).astype(F32))
             for r in range(R):
                 wide[at(j, C), 128 * r : 128 * r + 128] = m[C * r : C * r + C]
     tall[...] = table_dot(ahead, wide[...])
     upper = lax.broadcasted_iota(jnp.int32, (8, 1), 0) < 4
+
+    def tile(p, r, offset):
+        return tall[at(p, 16, 8, offset), 128 * r : 128 * r + 128]
+
+    def fours(p, i):
+        return jnp.where(upper, tile(p, 2 * i, 8), tile(p, 2 * i + 1, 8))
+
     for group in tos:
         for p in group:
-            def rows(r, offset):
-                return tall[at(p, 16, 8, offset), 128 * r : 128 * r + 128]
-            t = [rows(r, 0) for r in range(R)]
-            t += [jnp.where(upper, rows(2 * i, 8), rows(2 * i + 1, 8)) for i in range(3)]
-            put(p, pack_lat(t))
-        put.send(group)
-
-
-def slot_rows(kc, eights, fours):
-    if kc < 8:
-        return eights, pl.ds(kc, H, stride=8)
-    return fours, pl.ds(kc - 8, H, stride=4)
-
-
-def height_ahead(froms, recv, eights, fours, wide, spec, fwd, fwd0):
-    for group in froms:
-        recv.wait(group)
-        for p in group:
-            t = unpack_lat(recv(p).astype(F32))
-            eights[at(p, 48), :] = jnp.concatenate(t[:6], axis=0)
-            fours[at(p, 24), :] = jnp.concatenate(t[6:], axis=0)
-    for c in range(2):
-        for k in range(KS):
-            ref, rows = slot_rows(c * KS + k, eights, fours)
-            wide[H * c : H * c + H, 128 * k : 128 * k + 128] = ref[rows, :]
-    zero = table_dot(fwd0, wide[:, 0:128])
-    rest = table_dot(fwd, wide[:, 128:])
-    half = KS * H
-    spec[0:H, 0:128] = zero[0:H]
-    spec[0:H, 128:256] = zero[H : 2 * H]
-    spec[half : half + H, 0:128] = zero[2 * H : 3 * H]
-    spec[half : half + H, 128:256] = zero[3 * H :]
-    for k in range(1, KS):
-        real, imag = rest[0:H, 128 * (k - 1) : 128 * k], rest[H:, 128 * (k - 1) : 128 * k]
-        spec[H * k : H * k + H, 0:128] = real
-        spec[H * k : H * k + H, 128:256] = imag
-        spec[half + H * k : half + H * k + H, 0:128] = real
-        spec[half + H * k : half + H * k + H, 128:256] = -imag
-
-
-def height_back(spec, eights, fours, wide, first, inv, inv0, tos, put):
-    half = KS * H
-    for i, (start, lane) in enumerate(((0, 0), (0, 128), (half, 0), (half, 128))):
-        first[H * i : H * i + H, :] = spec[start : start + H, lane : lane + 128]
-    for k in range(1, KS):
-        low = spec[H * k : H * k + H, :]
-        high = spec[half + H * k : half + H * k + H, :]
-        wide[0:H, 128 * k : 128 * k + 128] = low[:, 0:128] + high[:, 0:128]
-        wide[H : 2 * H, 128 * k : 128 * k + 128] = low[:, 128:] - high[:, 128:]
-    zero = table_dot(inv0, first[...])
-    rest = table_dot(inv, wide[:, 128:])
-    for c in range(2):
-        for k in range(KS):
-            ref, rows = slot_rows(c * KS + k, eights, fours)
-            values = zero[H * c : H * c + H] if k == 0 else rest[H * c : H * c + H, 128 * (k - 1) : 128 * k]
-            ref[rows, :] = values
+            put(p, pack_out(0, [tile(p, r, 0) for r in range(R)], [None, None, fours(p, 2)]))
+        put.send(group, 0, OUT, 0)
     for group in tos:
         for p in group:
-            t = [eights[at(p, 48, 8, 8 * i), :] for i in range(6)]
-            t += [fours[at(p, 24, 8, 8 * i), :] for i in range(3)]
-            put(p, pack_lat(t))
-        put.send(group)
+            put(p, pack_out(1, None, [fours(p, i) for i in range(3)]), OUT)
+        put.send(group, OUT, 56 - OUT, 1)
+
+
+def slot_rows(c, k, eights, fours):
+    if k < 4:
+        return eights, pl.ds(4 * c + k, H, stride=8)
+    return fours, pl.ds(2 * c + k - 4, H, stride=4)
+
+
+def spec_rows(k, high):
+    start = H * (k + 4 * high) if k < 4 else H * (8 + (k - 4) + 2 * high)
+    return slice(start, start + H)
+
+
+PARTS = ((0, 8 * H), (8 * H, 12 * H))
+SLOTS = ((0, 1, 2, 3), (4, 5))
+
+
+def height_ahead(part, froms, recv, eights, fours, spec, fwd, fwd0):
+    recv.wait(NP - 1, *((0, OUT), (OUT, 56 - OUT))[part], part)
+    for p in froms:
+        t = unpack_out(part, eight_rows(recv(p, 0, 56 if part else OUT).astype(F32)))
+        if part == 0:
+            eights[at(p, 48), :] = jnp.concatenate(t, axis=0)
+        else:
+            fours[at(p, 24), :] = jnp.concatenate(t, axis=0)
+
+    def column(k):
+        pair = [slot_rows(c, k, eights, fours) for c in range(2)]
+        return jnp.concatenate([ref[rows, :] for ref, rows in pair], axis=0).astype(BF16)
+
+    slots = SLOTS[part]
+    if part == 0:
+        zero = table_dot(fwd0, column(0))
+        for i in range(4):
+            spec[spec_rows(0, i // 2), 128 * (i % 2) : 128 * (i % 2) + 128] = zero[H * i : H * i + H]
+        slots = slots[1:]
+    rest = table_dot(fwd, jnp.concatenate([column(k) for k in slots], axis=1))
+    for i, k in enumerate(slots):
+        real, imag = rest[0:H, 128 * i : 128 * i + 128], rest[H:, 128 * i : 128 * i + 128]
+        for high in range(2):
+            spec[spec_rows(k, high), 0:128] = real
+            spec[spec_rows(k, high), 128:256] = -imag if high else imag
+
+
+def height_back(part, spec, eights, fours, inv, inv0, tos, put):
+    def column(k):
+        low, high = spec[spec_rows(k, 0), :], spec[spec_rows(k, 1), :]
+        real, imag = low[:, 0:128] + high[:, 0:128], low[:, 128:] - high[:, 128:]
+        return jnp.concatenate([real, imag], axis=0).astype(BF16)
+
+    def keep(k, values):
+        for c in range(2):
+            ref, rows = slot_rows(c, k, eights, fours)
+            ref[rows, :] = values[H * c : H * c + H]
+
+    slots = SLOTS[part]
+    if part == 0:
+        places = [spec[spec_rows(0, i // 2), 128 * (i % 2) : 128 * (i % 2) + 128] for i in range(4)]
+        keep(0, table_dot(inv0, jnp.concatenate(places, axis=0)))
+        slots = slots[1:]
+    rest = table_dot(inv, jnp.concatenate([column(k) for k in slots], axis=1))
+    for i, k in enumerate(slots):
+        keep(k, rest[:, 128 * i : 128 * i + 128])
+    for group in tos:
+        for p in group:
+            a = [eights[at(p, 48, 8, 8 * i), :] for i in range(6)]
+            c = [fours[at(p, 24, 8, 8 * i), :] for i in range(3)] if part else None
+            put(p, pack_back(part, a, c), BACK * part)
+        put.send(group, *((0, BACK), (BACK, 56 - BACK))[part], part)
 
 
 def width_back(froms, recv, tall, wide, even, odd, tos, put):
-    for group in froms:
-        recv.wait(group)
-        for p in group:
-            t = unpack_lat(recv(p).astype(F32))
-            for r in range(R):
-                lane = 128 * (r // 2) + 384 * (r % 2)
-                tall[at(p, 16, 8), lane : lane + 128] = t[r]
-                tall[at(p, 16, 8, 8), lane : lane + 128] = t[6 + r // 2]
+    def keep(p, r, offset, tile):
+        lane = 128 * (r // 2) + 384 * (r % 2)
+        tall[at(p, 16, 8, offset), lane : lane + 128] = tile
+
+    recv.wait(NP - 1, 0, BACK, 0)
+    for p in froms:
+        t = eight_rows(recv(p, 0, BACK).astype(F32))
+        for r, tile in enumerate(t + [from_beside(*t[:3])]):
+            keep(p, r, 0, tile)
+    recv.wait(NP - 1, BACK, 56 - BACK, 1)
+    for p in froms:
+        t = eight_rows(recv(p, BACK - 8, 64 - BACK).astype(F32))
+        keep(p, 5, 0, from_beside(*t[:3]))
+        for r in range(R):
+            keep(p, r, 8, t[1 + r // 2])
     wide[:, 0:384] = table_dot(even, tall[:, 0:384])
     wide[:, 384:768] = table_dot(odd, tall[:, 384:768])
-    for group in tos:
+    for half, group in enumerate(tos):
         for j in group:
             m = [wide[at(j, C), 128 * (r // 2) + 384 * (r % 2) : 128 * (r // 2) + 384 * (r % 2) + 128] for r in range(R)]
             put(j, pack_lon(jnp.concatenate(m, axis=0)))
-        put.send(group)
+        put.send(group, 0, 112, half)
 
 
 def gathered(recv):
-    recv.wait(range(NJ // 2))
-    recv.wait(range(NJ // 2))
+    for half in range(2):
+        recv.wait(NJ // 2, 0, 112, half)
     return joined_blocks([unpack_lon(recv(b).astype(F32))[:, 0:128] for b in range(NJ)])
 
 
@@ -291,9 +338,9 @@
 CHUNK = 384
 
 
-def spectral_ahead(spec, first_pre, squares, mat1, bias1, mat2, bias2):
-    for i in range(ROWS // CHUNK):
-        rows = slice(i * CHUNK, i * CHUNK + CHUNK)
+def spectral_ahead(part, spec, first_pre, squares, mat1, bias1, mat2, bias2):
+    for start in range(*PARTS[part], CHUNK):
+        rows = slice(start, start + CHUNK)
         pre = matrix_dot(spec[rows, :], mat1) + bias1[...]
         first_pre[rows, :] = pre
         second = matrix_dot(pre * cumulative(pre), mat2) + bias2[...]
@@ -309,9 +356,9 @@
         first_pre[rows, :] = cumulative(pre) + pre * density(pre)
 
 
-def spectral_adjoint(spec, slopes, squares, mat1, mat2):
-    for i in range(ROWS // CHUNK):
-        rows = slice(i * CHUNK, i * CHUNK + CHUNK)
+def spectral_adjoint(part, spec, slopes, squares, mat1, mat2):
+    for start in range(*PARTS[part], CHUNK):
+        rows = slice(start, start + CHUNK)
         grad = matrix_dot(spec[rows, :] * squares[rows, :], mat2)
         spec[rows, :] = matrix_dot(grad * slopes[rows, :], mat1)
 
@@ -381,7 +428,7 @@
         advanced, sensitivity, state, weight1, bias_1, weight2, bias_2, gain1, shift1, gain2, shift2, fc1, fc1_bias, fc2, fc2_bias, cotangent,
         ahead, fwd, even, odd, inv,
         lon_send, lon_recv, lat_send, lat_recv, lowered, mixed, grads, hidden, gh, acc,
-        wide, tall, eights, fours, first, spec, first_pre, squares, mat1, mat2, turned1, turned2, bias1, bias2, fwd0, inv0,
+        wide, tall, eights, fours, spec, first_pre, squares, mat1, mat2, turned1, turned2, bias1, bias2, fwd0, inv0,
         load_sem, store_sem, lon_send_sem, lon_recv_sem, lat_send_sem, lat_recv_sem,
     ) = rest
     p = lax.axis_index("lat")
@@ -405,16 +452,19 @@
     def device(axis, to):
         return {"lon": to, "ens": 1 - ens} if axis == "lon" else {"lat": to}
 
+    held_here = (
+        state, weight1, bias_1, weight2, bias_2, gain1, shift1, gain2, shift2, fc1, fc1_bias, fc2, fc2_bias, cotangent,
+        ahead, fwd, even, odd, inv,
+    )
+    loads = [pltpu.make_async_copy(a, b, load_sem.at[i + 1]) for i, (a, b) in enumerate(zip(sources, held_here))]
+    state_loads = [pltpu.make_async_copy(sources[0].at[s], state.at[s], load_sem.at[s]) for s in range(2)]
+    for load in state_loads[:1] + [loads[i] for i in FIRST] + state_loads[1:]:
+        load.start()
     barrier = pltpu.get_barrier_semaphore()
     for axis, peers in (("lat", lat_to), ("lon", lon_to)):
         for to in peers:
             pl.semaphore_signal(barrier, inc=1, device_id=device(axis, to), device_id_type=pl.DeviceIdType.MESH)
-    held_here = (
-        state, weight1, bias_1, weight2, bias_2, gain1, shift1, gain2, shift2, fc1, fc1_bias, fc2, fc2_bias, cotangent,
-        ahead, fwd, even, odd, inv,
-    )
-    loads = [pltpu.make_async_copy(a, b, load_sem.at[i]) for i, (a, b) in enumerate(zip(sources, held_here))]
-    for i in FIRST + MIDDLE + LAST:
+    for i in MIDDLE + LAST:
         loads[i].start()
     for i in FIRST:
         loads[i].wait()
@@ -425,57 +475,54 @@
             return lon_send, lon_recv, lon_send_sem, lon_recv_sem, e, j
         return lat_send, lat_recv, lat_send_sem, lat_recv_sem, e, p
 
-    def copy(x, s, axis, to, half):
+    def copy(x, s, axis, to, start, rows, part):
         send, recv, send_sem, recv_sem, e, me = buffers(x, s, axis)
         return pltpu.make_async_remote_copy(
-            src_ref=send.at[e, to],
-            dst_ref=recv.at[e, me],
+            src_ref=send.at[e, to, pl.ds(start, rows)],
+            dst_ref=recv.at[e, me, pl.ds(start, rows)],
             send_sem=send_sem.at[e],
-            recv_sem=recv_sem.at[e, half],
+            recv_sem=recv_sem.at[e, part],
             device_id=device(axis, to),
             device_id_type=pl.DeviceIdType.MESH,
         )
 
-    def several(x, s, axis, count, half):
+    def several(x, s, axis, count, start, rows, part):
         send, recv, send_sem, recv_sem, e, me = buffers(x, s, axis)
         return pltpu.make_async_remote_copy(
-            src_ref=send.at[e, pl.ds(0, count)],
-            dst_ref=recv.at[e, pl.ds(0, count)],
+            src_ref=send.at[e, pl.ds(0, count), pl.ds(start, rows)],
+            dst_ref=recv.at[e, pl.ds(0, count), pl.ds(start, rows)],
             send_sem=send_sem.at[e],
-            recv_sem=recv_sem.at[e, half],
+            recv_sem=recv_sem.at[e, part],
             device_id=device(axis, lon_to[0] if axis == "lon" else lat_to[0]),
             device_id_type=pl.DeviceIdType.MESH,
         )
 
-    class Sender:
+    class sender:
         def __init__(self, x, s, axis):
-            self.where, self.half = (x, s, axis), 0
-
-        def __call__(self, to, values):
+            self.where = (x, s, axis)
+
+        def __call__(self, to, values, start=0):
             send, recv, _, _, e, _ = buffers(*self.where)
-            (recv if to is p else send)[e, to] = values.astype(BF16)
-
-        def send(self, group):
+            (recv if to is p else send)[e, to, start : start + values.shape[0]] = values.astype(BF16)
+
+        def send(self, group, start, rows, part):
             for to in group:
                 if to is not p:
-                    copy(*self.where, to, self.half).start()
-            self.half += 1
-
-    class Receiver:
+                    copy(*self.where, to, start, rows, part).start()
+
+    class receiver:
         def __init__(self, x, s, axis):
-            self.where, self.half = (x, s, axis), 0
-
-        def wait(self, group):
-            several(*self.where, len([0 for source in group if source is not p]), self.half).wait_recv()
-            self.half += 1
-
-        def __call__(self, source):
+            self.where = (x, s, axis)
+
+        def wait(self, count, start, rows, part):
+            several(*self.where, count, start, rows, part).wait_recv()
+
+        def __call__(self, source, start=0, rows=112):
             _, recv, _, _, e, _ = buffers(*self.where)
-            return recv[e, source]
-
-    sender, receiver = Sender, Receiver
+            return recv[e, source, start : start + rows]
+
     lon_tos, lon_froms = [lon_to[:4], lon_to[4:]], [lon_from[:4], lon_from[4:]]
-    lat_tos, lat_froms = [lat_to[:8], lat_to[8:] + [p]], [[p] + lat_from[:8], lat_from[8:]]
+    lat_tos, lat_froms = [lat_to[:8], lat_to[8:] + [p]], [p] + lat_from
 
     def tokens(ref, s):
         return jnp.concatenate([ref[s, r].astype(F32) for r in range(R)], axis=0)
@@ -495,13 +542,23 @@
             pl.semaphore_wait(barrier, NP - 1 + NJ)
         for half in range(2):
             for to in lon_tos[half]:
-                copy(x, s, "lon", to, half).start()
-
-    for s in range(2):
+                copy(x, s, "lon", to, 0, 112, half).start()
+
+    def first_norm(s):
         with jax.named_scope("ln"):
+            state_loads[s].wait()
             normed, _ = layer_norm(tokens(state, s))
             lowered[s] = (normed * row(gain1) + row(shift1)).astype(BF16).astype(F32)
             send_tokens(0, s, lowered)
+
+    def cot_product(start, stop):
+        with jax.named_scope("gh"):
+            cots = jnp.concatenate([tokens(cotangent, s) for s in range(2)], axis=0).astype(BF16)
+            for n in range(start, stop):
+                cols = slice(n * HC, n * HC + HC)
+                gh[:, cols] = dot_nt(cots, fc2[cols, :])
+
+    first_norm(0)
     for i in MIDDLE:
         loads[i].wait()
     fill_matrix(mat1, weight1)
@@ -511,27 +568,25 @@
     fill_bias(bias1, bias_1)
     fill_bias(bias2, bias_2)
     fill_first(fwd0, inv0, fwd, inv, p == 0)
+    loads[11].wait()
+    cot_product(0, 2)
+    first_norm(1)
+    cot_product(2, 4)
 
     for s in range(2):
         with jax.named_scope("w0"):
             width_ahead(lon_froms, receiver(0, s, "lon"), wide, tall, ahead, lat_tos, sender(0, s, "lat"))
-
-    with jax.named_scope("gh"):
-        loads[11].wait()
-        cots = jnp.concatenate([tokens(cotangent, s) for s in range(2)], axis=0).astype(BF16)
-
-        def cot_step(n):
-            cols = pl.ds(pl.multiple_of(n * HC, HC), HC)
-            gh[:, cols] = dot_nt(cots, fc2[cols, :])
-        loop(FF // HC, cot_step)
-
-    for s in range(2):
-        with jax.named_scope("h0"):
-            height_ahead(lat_froms, receiver(0, s, "lat"), eights, fours, wide, spec, fwd, fwd0)
-        with jax.named_scope("sp0"):
-            spectral_ahead(spec, first_pre.at[s], squares.at[s], mat1, bias1, mat2, bias2)
-        with jax.named_scope("hb1"):
-            height_back(spec, eights, fours, wide, first, inv, inv0, lat_tos, sender(1, s, "lat"))
+    cot_product(4, 6)
+
+    for s in range(2):
+        get, put = receiver(0, s, "lat"), sender(1, s, "lat")
+        for part in range(2):
+            with jax.named_scope(f"h0{part}"):
+                height_ahead(part, lat_froms, get, eights, fours, spec, fwd, fwd0)
+            with jax.named_scope(f"sp0{part}"):
+                spectral_ahead(part, spec, first_pre.at[s], squares.at[s], mat1, bias1, mat2, bias2)
+            with jax.named_scope(f"hb1{part}"):
+                height_back(part, spec, eights, fours, inv, inv0, lat_tos, put)
     for s in range(2):
         with jax.named_scope("slopes"):
             spectral_slopes(first_pre.at[s])
@@ -569,12 +624,14 @@
             advance(s)
         store(0, s).start()
     for s in range(2):
-        with jax.named_scope("h2"):
-            height_ahead(lat_froms, receiver(2, s, "lat"), eights, fours, wide, spec, fwd, fwd0)
-        with jax.named_scope("sp2"):
-            spectral_adjoint(spec, first_pre.at[s], squares.at[s], turned1, turned2)
-        with jax.named_scope("hb3"):
-            height_back(spec, eights, fours, wide, first, inv, inv0, lat_tos, sender(3, s, "lat"))
+        get, put = receiver(2, s, "lat"), sender(3, s, "lat")
+        for part in range(2):
+            with jax.named_scope(f"h2{part}"):
+                height_ahead(part, lat_froms, get, eights, fours, spec, fwd, fwd0)
+            with jax.named_scope(f"sp2{part}"):
+                spectral_adjoint(part, spec, first_pre.at[s], squares.at[s], turned1, turned2)
+            with jax.named_scope(f"hb3{part}"):
+                height_back(part, spec, eights, fours, inv, inv0, lat_tos, put)
     for s in range(2):
         with jax.named_scope("wb3"):
             width_back(lat_froms, receiver(3, s, "lat"), tall, wide, even, odd, lon_tos, sender(3, s, "lon"))
@@ -588,17 +645,30 @@
     with jax.named_scope("tail_sent"):
         for x in range(4):
             for s in range(2):
-                several(x, s, "lon", NJ, 0).wait_send()
-                several(x, s, "lat", NP - 1, 0).wait_send()
+                several(x, s, "lon", NJ, 0, 112, 0).wait_send()
+                several(x, s, "lat", NP - 1, 0, 56, 0).wait_send()
     with jax.named_scope("tail_store"):
         for i in range(2):
             for s in range(2):
                 store(i, s).wait()
 
 
-def finish(advanced, sensitivity, advanced_out, sensitivity_out):
-    advanced_out[...] = advanced[...]
-    sensitivity_out[...] = sensitivity[...]
+def finish(advanced, sensitivity, advanced_out, sensitivity_out, held, sem):
+    pieces = [(i, s, slice(3 * h, 3 * h + 3)) for i in range(2) for s in range(2) for h in range(2)]
+    arrays = ((advanced, advanced_out), (sensitivity, sensitivity_out))
+    come = [
+        pltpu.make_async_copy(arrays[i][0].at[s, r], held.at[i, s, r], sem.at[0, n]) for n, (i, s, r) in enumerate(pieces)
+    ]
+    leave = [
+        pltpu.make_async_copy(held.at[i, s, r], arrays[i][1].at[s, r], sem.at[1, n]) for n, (i, s, r) in enumerate(pieces)
+    ]
+    for copy in come:
+        copy.start()
+    for arriving, leaving in zip(come, leave):
+        arriving.wait()
+        leaving.start()
+    for copy in leave:
+        copy.wait()
 
 
 def shards(
@@ -637,7 +707,6 @@
             pltpu.VMEM((16 * NP, D), F32),
             pltpu.VMEM((8 * H, 128), F32),
             pltpu.VMEM((4 * H, 128), F32),
-            pltpu.VMEM((4 * H, 128), F32),
             pltpu.VMEM((ROWS, 256), F32),
             pltpu.VMEM((2, ROWS, 256), F32),
             pltpu.VMEM((2, ROWS, 256), F32),
@@ -649,7 +718,7 @@
             pltpu.VMEM((1, 256), F32),
             pltpu.VMEM((2, 4 * H, 2 * H), BF16),
             pltpu.VMEM((2 * H, 4 * H), BF16),
-            pltpu.SemaphoreType.DMA((len(operands),)),
+            pltpu.SemaphoreType.DMA((len(operands) + 1,)),
             pltpu.SemaphoreType.DMA((4,)),
             pltpu.SemaphoreType.DMA((8,)),
             pltpu.SemaphoreType.DMA((8, 2)),
@@ -664,8 +733,9 @@
     return pl.pallas_call(
         finish,
         out_shape=(out, out),
-        in_specs=[vmem, vmem],
-        out_specs=(vmem, vmem),
+        in_specs=[hbm, hbm],
+        out_specs=(hbm, hbm),
+        scratch_shapes=[pltpu.VMEM((2, *state.shape), BF16), pltpu.SemaphoreType.DMA((2, 8))],
         compiler_params=pltpu.CompilerParams(vmem_limit_bytes=67043328),
         name="finish",
     )(*results)

time: 83 us -> 84.4 us (1.017)
  Pallas kernels: 82.2 us -> 83.5 us
    pallas_call x1, Pallas kernels: 80.2 us -> 81.5 us  [shards(): pl.pallas_call(kernel, out_shape=(out, out), in_specs=specs, out_specs=(h...]
where the time goes in v3:
time: 84.4 us; the launch traced here: 84.3 us
  Pallas kernels  83.5 us (99%)
    pallas_call x1, Pallas kernels, shards(): pl.pallas_call(kernel, out_shape=(out, out), in_specs=specs, out_specs=(h...  81.5 us
    pallas_call x1, Pallas kernels, shards(): pl.pallas_call(finish, out_shape=(out, out), in_specs=[hbm, hbm], out_spe...  2.03 us

profile of v3, /device:TPU:1, one launch (start us, length us, event | category | flops | bytes accessed | tf_op | source)
XLA Modules:
  0.0 84.3 jit_solution(15864271990036409261)
XLA Ops:
  0.6 81.5 %block.1 = (bf16[2,6,24,768]{3,2,1,0:T(8,128)(2,1)}, bf16[2,6,24,768]{3,2,1,0:T(8,128)(2,1)}) custom-call(bf16[2,6,24,768]{3,2,1,0:T(8,128)(2,1)} %refs_0_.1, f32[2,1,96,96]{3,2,1,0:T(8,128)} %refs_1_.1, f32[2,1,96]{2,1,0:T(1,128)} %refs_2_.1, f32[2,1,96,96]{3,2,1,0:T(8,128)} %refs_3_.1, f32[2,1,96]{2,1,0:T(1,128)} %refs_4_.1, f32[768]{0:T(1024)} %refs_5_.1, ...), custom_call_target="tpu_custom_call" | custom-call | tf_op jit(solution)/shard_map/block/pallas_call | solution.py:687
  82.1 2.0 %finish.1 = (bf16[2,6,24,768]{3,2,1,0:T(8,128)(2,1)}, bf16[2,6,24,768]{3,2,1,0:T(8,128)(2,1)}) custom-call(bf16[2,6,24,768]{3,2,1,0:T(8,128)(2,1)} %get-tuple-element.4.advanced, bf16[2,6,24,768]{3,2,1,0:T(8,128)(2,1)} %get-tuple-element.5.sensitivity), custom_call_target="tpu_custom_call" | custom-call | tf_op jit(solution)/shard_map/finish/pallas_call | solution.py:733
